TPU v7x, 256 devices: a whole 4x4x8 slice. The times are simulated.
256 devices in a mesh: grp: 32 (over z, x), dom: 8 (over y, core).
Axes of the slice: x: 4, y: 4, z: 8, core: 2. Of those that a mesh axis runs over, the one named last changes fastest.
Arguments:
- positions: float32 [3, 32768, 512], P(None, ('grp', 'dom')), may hold values from 0 to 1
- velocities: float32 [3, 32768, 512], P(None, ('grp', 'dom')), may hold values from -6 to 6
- masses: float32 [32768, 512], P(('grp', 'dom')), may hold values from 0.5 to 2
- block_halo: int32 [32768], P(('grp', 'dom')), may hold values from 0 to 32767, as said below
- block_shift: int32 [3, 32768], P(None, ('grp', 'dom')), may hold values from -1 to 1
- block_live: int32 [32768], P(('grp', 'dom')), may hold values from 64 to 512
- block_count: int32 [256], P(('grp', 'dom')), may hold values from 32 to 128
- home_slot: int32 [32768], replicated, may hold values from 0 to 32767, as said below
Outputs:
- halo_table: float32 [11, 32768], P(None, ('grp', 'dom'))
- kinetic: float32 [32768, 512], P(('grp', 'dom'))
- radial: float32 [32768, 512], P(('grp', 'dom'))
Inputs may be any that keep to these rules, and one draw needn't show every extreme that they name: A permutation: the halo h is owned by the device of index home_slot[h] // 128 (grp+dom order), in its column home_slot[h] % 128. `block_halo`: the owner of a block's halo lies in the block's own index of grp or in the next one (index + 1, wrapping around); both occur.
All inputs are finite; a program needn't handle non-finite values.
Results may differ from a plain program's by a relative error of at most 0.0003.
Values sent between devices are 32-bit elements; how exact they have to be, the bound alone decides.
A program may use at most 64 MiB of HBM per device.

v0:
```python
import functools

import jax
import jax.numpy as jnp
from jax import lax
from jax.sharding import Mesh
from jax.sharding import PartitionSpec as P

GRP_DOM = ("grp_0", "grp_1", "dom_0", "dom_1")
DOM = ("dom_0", "dom_1")
GRP = ("grp_0", "grp_1")


BOX = 1.0
EPSILON = 1e-06


def over_axes(shard, axes):
    return functools.reduce(lax.psum, axes, shard)


def in_blocks(shard, dim, devices):
    dims = shard.shape
    pieces = shard.reshape(*dims[:dim], devices, dims[dim] // devices, *dims[dim + 1 :])
    return jnp.moveaxis(pieces, dim, 0)


def summed_on_arrival(shard, axis, dim):
    pieces = in_blocks(shard, dim, lax.axis_size(axis))
    arrived = lax.all_to_all(pieces, axis, split_axis=0, concat_axis=0, tiled=True)
    return arrived.sum(axis=0)


def from_behind(shard, axis, by):
    devices = lax.axis_size(axis)
    return lax.ppermute(shard, axis, [(i, (i + by) % devices) for i in range(devices)])


def in_order(pieces, dim):
    dims = list(pieces.shape[1:])
    dims[dim] *= pieces.shape[0]
    return jnp.moveaxis(pieces, 0, dim).reshape(dims)


def sent_to_all(shard, axis):
    devices = lax.axis_size(axis)
    return lax.all_to_all(
        jnp.broadcast_to(shard[None], (devices, *shard.shape)), axis, 0, 0, tiled=True
    )


def collect(shard, axis, dim):
    return in_order(sent_to_all(shard, axis), dim)


def crossed(first, second):
    return jnp.stack(
        [
            first[1] * second[2] - first[2] * second[1],
            first[2] * second[0] - first[0] * second[2],
            first[0] * second[1] - first[1] * second[0],
        ]
    )


def block_moments(positions, velocities, masses, block_shift, block_live, valid):
    lanes = jnp.arange(masses.shape[1], dtype=jnp.int32)
    live_mask = ((lanes[None, :] < block_live[:, None]) & valid[:, None]).astype(masses.dtype)
    weights = masses * live_mask
    unwrapped = positions + BOX * block_shift.astype(positions.dtype)[:, :, None]
    speed_sq = jnp.sum(velocities * velocities, axis=0)
    angular = crossed(unwrapped, velocities)
    rows = [
        jnp.sum(weights, axis=1)[None],
        jnp.sum(weights * unwrapped, axis=2),
        jnp.sum(weights * velocities, axis=2),
        jnp.sum(weights * speed_sq, axis=1)[None],
        jnp.sum(weights * angular, axis=2),
    ]
    return (jnp.concatenate(rows, axis=0), live_mask, unwrapped)


def halo_properties(sums, total, halos):
    heavy = jnp.maximum(sums[0], 1.0)
    centre = sums[1:4] / heavy
    drift = sums[4:7] / heavy
    spread = sums[7] / heavy - jnp.sum(drift * drift, axis=0)
    spin = sums[8:11] / heavy - crossed(centre, drift)
    share = sums[0] * halos / total
    return jnp.concatenate([share[None], centre, drift, spread[None], spin], axis=0)


def particle_outputs(unwrapped, velocities, live_mask, stats):
    centre = stats[0:3][:, :, None]
    drift = stats[3:6][:, :, None]
    spread = stats[6][:, None]
    offset = velocities - drift
    kinetic = jnp.sum(offset * offset, axis=0) / (3.0 * spread + EPSILON)
    distance = unwrapped - centre
    radial = jnp.sum(distance * distance, axis=0)
    return (kinetic * live_mask, radial * live_mask)


def local(
    positions, velocities, masses, block_halo, block_shift, block_live, block_count, home_slot
):
    blocks = masses.shape[0]
    halos = home_slot.shape[0]
    owned_count = halos // lax.axis_size(GRP_DOM)
    valid = jnp.arange(blocks, dtype=jnp.int32) < block_count[0]
    moments, live_mask, unwrapped = block_moments(
        positions, velocities, masses, block_shift, block_live, valid
    )
    slots = home_slot[block_halo]
    domains = lax.axis_size(DOM)
    slab_groups = lax.axis_size(GRP)
    window = domains * owned_count
    owner = slots // owned_count
    relative = (owner // domains - lax.axis_index(GRP)) % slab_groups
    local_column = relative * window + owner % domains * owned_count + slots % owned_count
    table = jnp.zeros((11, 2 * window), jnp.float32).at[:, local_column].add(moments)
    total = over_axes(jnp.sum(moments[0]), GRP_DOM)
    ordered = (
        table.reshape(11, 2, domains, owned_count).transpose(0, 2, 1, 3).reshape(11, 2 * window)
    )
    shares = summed_on_arrival(ordered, DOM, 1)
    arrived = from_behind(shares[:, owned_count:], GRP, 1)
    owned_sums = shares[:, :owned_count] + arrived
    halo_table = halo_properties(owned_sums, total, halos)
    own_stats = halo_table[1:8]
    returned = from_behind(own_stats, GRP, -1)
    both = collect(jnp.stack([own_stats, returned], axis=0), DOM, 2)
    stats = jnp.concatenate([both[0], both[1]], axis=1)[:, local_column]
    kinetic, radial = particle_outputs(unwrapped, velocities, live_mask, stats)
    return (halo_table, kinetic, radial)


def solution(mesh):
    finer = Mesh(mesh.devices.reshape(8, 4, 4, 2), ("grp_0", "grp_1", "dom_0", "dom_1"))
    placed = (
        P(None, GRP_DOM, None),
        P(None, GRP_DOM, None),
        P(GRP_DOM, None),
        P(GRP_DOM),
        P(None, GRP_DOM),
        P(GRP_DOM),
        P(GRP_DOM),
        P(),
    )
    return jax.shard_map(
        local,
        mesh=finer,
        in_specs=placed,
        out_specs=(P(None, GRP_DOM), P(GRP_DOM, None), P(GRP_DOM, None)),
        check_vma=False,
    )
```

profile of v0, /device:TPU:1, one launch (start us, length us, event | category | flops | bytes accessed | tf_op | source)
XLA Modules:
  0.0 82.5 jit_solution(17053118554432368743)
XLA Ops:
  0.6 0.0 copy-start
  0.6 0.7 convert_element_type.4
  2.0 0.0 copy-start.2
  2.0 1.3 %broadcast_add_fusion = f32[3,128,512]{2,1,0:T(8,128)S(1)} fusion(f32[3,128,512]{2,1,0:T(8,128)} %param.8, f32[3,128]{1,0:T(4,128)S(1)} %convert_element_type.4), kind=kLoop, calls=%fused_computation.12 | loop fusion | flops 196608 | bytes 1574400 | tf_op jit(solution)/shard_map/add | solution.py:70
  3.4 0.0 copy-done.2
  3.4 0.0 copy-start.3
  3.4 0.0 copy-start.4
  3.4 0.0 copy-start.1
  3.4 0.2 multiply_subtract_fusion.2
  3.6 0.8 copy-done.3
  4.4 0.0 copy-done.4
  4.4 0.1 fusion.5
  4.5 0.2 copy-done.1
  4.6 0.4 multiply_reduce_fusion.2
  5.0 0.8 fusion.16
  5.9 0.1 copy.29
  6.0 0.0 copy-start.5
  6.0 0.6 copy-done.5
  6.7 0.0 copy-done
  6.7 1.1 %gather_fusion = s32[128]{0:T(128)S(1)} fusion(s32[32768]{0:T(1024)S(1)} %copy-done, s32[1024]{0:T(1024)S(1)} %pad_clamp_fusion.1), kind=kCustom, calls=%fused_computation | custom fusion | bytes 1536 | tf_op jit(solution)/shard_map/gather | solution.py:114
  7.9 1.3 %scatter_custom_fusion = f32[11,2048]{0,1:T(8,128)S(1)} fusion(s32[128]{0:T(128)S(1)} %fusion.13, f32[128,11]{1,0:T(8,128)S(1)} %copy.29, f32[]{:T(128)} %constant.70.clone.1), kind=kCustom, calls=%fused_computation.10 | custom fusion | flops 1408 | bytes 90116 | tf_op jit(solution)/shard_map/scatter-add | solution.py:121
  9.1 0.3 copy.30
  9.5 0.7 copy.31
  10.2 6.5 %all-to-all-start = ((f32[8,11,256]{2,1,0:T(8,128)}), f32[8,11,256]{2,1,0:T(8,128)S(1)}, u32[]{:S(2)}, u32[]{:S(2)}) async-start(f32[8,11,256]{2,1,0:T(8,128)} %copy.31), calls=%async_computation | async-start | bytes 262144 | tf_op jit(solution)/shard_map/all_to_all | solution.py:30
  16.6 16.6 %psum.28 = f32[]{:T(128)} all-reduce(f32[]{:T(128)} %get-tuple-element.7), channel_id=1, replica_groups=mesh['grp_0'=8,'grp_1'=4,'dom_0'=4,'dom_1'=2] {'grp_0'}, use_global_device_ids=true, to_apply=%region_9.10 | all-reduce | flops 1 | bytes 8 | tf_op jit(solution)/shard_map/psum | solution.py:19
  33.3 9.1 %psum.29 = f32[]{:T(128)} all-reduce(f32[]{:T(128)} %psum.28), channel_id=1, replica_groups=mesh['grp_0'=8,'grp_1'=4,'dom_0'=4,'dom_1'=2] {'grp_1'}, use_global_device_ids=true, to_apply=%region_10.11 | all-reduce | flops 1 | bytes 8 | tf_op jit(solution)/shard_map/psum | solution.py:19
  42.4 9.1 %psum.30 = f32[]{:T(128)} all-reduce(f32[]{:T(128)} %psum.29), channel_id=1, replica_groups=mesh['grp_0'=8,'grp_1'=4,'dom_0'=4,'dom_1'=2] {'dom_0'}, use_global_device_ids=true, to_apply=%region_11.12 | all-reduce | flops 1 | bytes 8 | tf_op jit(solution)/shard_map/psum | solution.py:19
  51.4 0.0 all-to-all-done
  51.5 0.1 collective-permute-start
  51.6 10.8 %psum.31 = f32[]{:T(128)} all-reduce(f32[]{:T(128)} %psum.30), channel_id=1, replica_groups=mesh['grp_0'=8,'grp_1'=4,'dom_0'=4,'dom_1'=2] {'dom_1'}, use_global_device_ids=true, to_apply=%region_12.13 | all-reduce | flops 1 | bytes 8 | tf_op jit(solution)/shard_map/psum | solution.py:19
  62.4 0.0 collective-permute-done
  62.4 0.7 fusion.14
  63.1 5.1 %collective-permute-start.1 = (f32[7,128]{1,0:T(8,128)S(1)}, f32[7,128]{1,0:T(8,128)S(1)}, u32[]{:S(2)}, u32[]{:S(2)}) collective-permute-start(f32[7,128]{1,0:T(8,128)S(1)} %pad_maximum_fusion.2), channel_id=1, source_target_pairs={{0,248},{8,0},{16,8},{24,16},{32,24},{40,32},{48,40},{56,48},{64,5... | collective-permute-start | bytes 10760 | tf_op jit(solution)/shard_map/ppermute | solution.py:36
  68.2 0.7 collective-permute-done.1
  69.0 0.6 broadcast_in_dim.14
  69.6 5.3 %all-to-all-start.1 = ((f32[8,2,7,128]{3,1,2,0:T(2,128)}), f32[8,2,7,128]{3,1,2,0:T(2,128)S(1)}, u32[]{:S(2)}, u32[]{:S(2)}) async-start(f32[8,2,7,128]{3,1,2,0:T(2,128)} %broadcast_in_dim.14), calls=%async_computation.1 | async-start | bytes 114688 | tf_op jit(solution)/shard_map/all_to_all | solution.py:47
  74.9 1.2 %concatenate.13 = f32[11,128]{1,0:T(8,128)} concatenate(f32[1,128]{1,0:T(1,128)S(1)} %get-tuple-element.21, f32[3,128]{1,0:T(4,128)S(1)} %get-tuple-element.19, f32[3,128]{1,0:T(4,128)S(1)} %get-tuple-element.11, f32[1,128]{1,0:T(1,128)S(1)} %get-tuple-element.20, f32[3,128]{1,0:T(4,128)S(1)} %divide_subtract_fusion), dimensions={0} | concatenate | bytes 11264 | tf_op jit(solution)/shard_map/concatenate | solution.py:90
  76.1 3.6 %all-to-all-done.1 = f32[8,2,7,128]{3,1,2,0:T(2,128)S(1)} async-done(((f32[8,2,7,128]{3,1,2,0:T(2,128)}), f32[8,2,7,128]{3,1,2,0:T(2,128)S(1)}, u32[]{:S(2)}, u32[]{:S(2)}) %all-to-all-start.1) | async-done | bytes 57376 | tf_op jit(solution)/shard_map/all_to_all | solution.py:47
  79.8 0.4 copy.35
  80.2 0.6 gather_fusion.1
  80.8 0.1 fusion.17
  80.9 0.2 fusion.7
  81.1 0.1 copy.37
  81.1 0.2 multiply_reduce_fusion
  81.4 0.1 copy.36
  81.4 0.2 multiply_reduce_fusion.1
  81.6 0.9 %fusion.4 = (f32[128,512]{1,0:T(8,128)}, f32[128,512]{1,0:T(8,128)}) fusion(f32[128,512]{1,0:T(8,128)S(1)} %multiply_reduce_fusion, s32[128]{0:T(128)S(1)} %copy-done.4, pred[128]{0:T(512)(128)(4,1)S(1)} %iota_compare_fusion.1, f32[128,512]{1,0:T(8,128)S(1)} %multiply_reduce_fusion.1, f32[128]{0:T(128)S(1)} %fusion.7), kind=kLoop, calls=%fused_computation.20 | loop fusion | flops 327680 | bytes 1049728 | tf_op jit(solution)/shard_map/mul | solution.py:101
  (22 shorter events, 0.3 us)
Async XLA Ops:
  0.6 6.0 %copy-start = (s32[32768]{0:T(1024)S(1)}, s32[32768]{0:T(1024)}, u32[]{:S(2)}) copy-start(s32[32768]{0:T(1024)} %param.15) | copy-start | bytes 393220
  2.0 1.4 %copy-start.2 = (f32[3,128,512]{2,1,0:T(8,128)S(1)}, f32[3,128,512]{2,1,0:T(8,128)}, u32[]{:S(2)}) copy-start(f32[3,128,512]{2,1,0:T(8,128)} %param.9) | copy-start | bytes 2359300
  3.4 0.9 %copy-start.3 = (f32[128,512]{1,0:T(8,128)S(1)}, f32[128,512]{1,0:T(8,128)}, u32[]{:S(2)}) copy-start(f32[128,512]{1,0:T(8,128)} %param.10) | copy-start | bytes 786436
  3.4 1.0 %copy-start.4 = (s32[128]{0:T(128)S(1)}, s32[128]{0:T(128)}, u32[]{:S(2)}) copy-start(s32[128]{0:T(128)} %param.13) | copy-start | bytes 1540
  3.4 1.2 %copy-start.1 = (f32[3,128,512]{2,1,0:T(8,128)S(1)}, f32[3,128,512]{2,1,0:T(8,128)}, u32[]{:S(2)}) copy-start(f32[3,128,512]{2,1,0:T(8,128)} %param.8) | copy-start | bytes 2359300
  6.0 0.7 copy-start.5
  10.2 41.3 %all-to-all-start = ((f32[8,11,256]{2,1,0:T(8,128)}), f32[8,11,256]{2,1,0:T(8,128)S(1)}, u32[]{:S(2)}, u32[]{:S(2)}) async-start(f32[8,11,256]{2,1,0:T(8,128)} %copy.31), calls=%async_computation | async-start | bytes 262144 | tf_op jit(solution)/shard_map/all_to_all | solution.py:30
  51.5 10.9 %collective-permute-start = (f32[11,128]{1,0:T(8,128)S(1)}, f32[11,128]{1,0:T(8,128)S(1)}, u32[]{:S(2)}, u32[]{:S(2)}) collective-permute-start(f32[11,128]{1,0:T(8,128)S(1)} %slice.121), channel_id=1, source_target_pairs={{0,8},{8,16},{16,24},{24,32},{32,40},{40,48},{48,56},{56,64},{64,7... | collective-permute-start | bytes 16904 | tf_op jit(solution)/shard_map/ppermute | solution.py:36
  63.1 5.9 %collective-permute-start.1 = (f32[7,128]{1,0:T(8,128)S(1)}, f32[7,128]{1,0:T(8,128)S(1)}, u32[]{:S(2)}, u32[]{:S(2)}) collective-permute-start(f32[7,128]{1,0:T(8,128)S(1)} %pad_maximum_fusion.2), channel_id=1, source_target_pairs={{0,248},{8,0},{16,8},{24,16},{32,24},{40,32},{48,40},{56,48},{64,5... | collective-permute-start | bytes 10760 | tf_op jit(solution)/shard_map/ppermute | solution.py:36
  69.6 10.1 %all-to-all-start.1 = ((f32[8,2,7,128]{3,1,2,0:T(2,128)}), f32[8,2,7,128]{3,1,2,0:T(2,128)S(1)}, u32[]{:S(2)}, u32[]{:S(2)}) async-start(f32[8,2,7,128]{3,1,2,0:T(2,128)} %broadcast_in_dim.14), calls=%async_computation.1 | async-start | bytes 114688 | tf_op jit(solution)/shard_map/all_to_all | solution.py:47
where the time goes:
time: 83 us; the launch traced here: 82.5 us
  blocking collectives  45.6 us (55%)
  starting transfers between devices  16.9 us (20%)
  local copies, waits for them, and re-layouts  7.11 us (9%)
  other arithmetic  7.06 us (9%)
  waiting for transfers between devices  4.36 us (5%)
  between operations  1.51 us (2%)
    psum x4, blocking collectives, over_axes(): return functools.reduce(lax.psum, axes, shard)  45.6 us
    all_to_all x1, starting transfers between devices, summed_on_arrival(): lax.all_to_all(pieces, axis, split_axis=0, concat_axis=0, tiled=True)  6.47 us
    all_to_all x1, starting transfers between devices, sent_to_all(): lax.all_to_all(jnp.broadcast_to(shard[None], (devices, *shard.shape)), ax...  5.26 us
    ppermute x2, starting transfers between devices, from_behind(): lax.ppermute(shard, axis, [(i, (i + by) % devices) for i in range(devices)])  5.18 us
    all_to_all x1, waiting for transfers between devices, sent_to_all(): lax.all_to_all(jnp.broadcast_to(shard[None], (devices, *shard.shape)), ax...  3.61 us
  transfers between devices with their start and end apart: 4, of which 2 were waited for; matrix products, arithmetic and copies ran while one was open for 2% of the time, Pallas kernels for 0%

commit v1 on v0

v1 whole, which is shorter than its diff:
```python
import functools

import jax
import jax.numpy as jnp
from jax import lax
from jax.experimental import pallas as pl
from jax.experimental.pallas import tpu as pltpu
from jax.sharding import PartitionSpec as P

MESH = pl.DeviceIdType.MESH
EPSILON = 1e-6
PLANE_GROUPS = 4
CHUNKS = 2
F32 = jnp.float32
NT = (((1,), (1,)), ((), ()))


def wrapped(index, size):
    return jnp.where(index >= size, index - size, index)


def iota(shape, dim):
    return lax.broadcasted_iota(jnp.int32, shape, dim)


def in_three(x):
    high = x.astype(jnp.bfloat16).astype(F32)
    rest = x - high
    middle = rest.astype(jnp.bfloat16).astype(F32)
    return jnp.concatenate([high, middle, rest - middle], axis=0)


def kernel(
    sizes,
    pos_hbm, vel_hbm, mass_hbm, halo_hbm, shift_hbm, live_hbm, count_hbm, slot_hbm,
    table_ref, kin_ref, rad_ref,
    pos, vel, mass, halo, shift, live, count, slots,
    live_bc, halo_bc, shift_bc, moments, extra, gather, plane, line,
    in_sem, small_sem, count_sem, send_sem, recv_sem,
):
    groups, domains, planes_groups = sizes
    blocks = mass.shape[0]
    width = mass.shape[1]
    depth = groups // planes_groups
    g, j = lax.axis_index("grp"), lax.axis_index("dom")
    z = g // planes_groups
    x = g - z * planes_groups
    nxt = wrapped(g + 1, groups)
    prv = jnp.where(g == 0, groups - 1, g - 1)

    order = sorted(range(domains), key=lambda k: -min(k, domains - k))
    near = [(grp, k, d) for grp, d in ((nxt, 0), (prv, 2)) for k in order]
    near += [(g, k, 1) for k in order if k]
    in_plane = [(a, k) for a in range(planes_groups) for k in range(domains) if (a, k) != (0, 0)]
    along = list(range(1, depth))

    def domain(k):
        return wrapped(j + k, domains)

    def plane_group(a):
        return z * planes_groups + wrapped(x + a, planes_groups)

    def line_group(a):
        return wrapped(z + a, depth) * planes_groups + x

    barrier = pltpu.get_barrier_semaphore()

    def greet(grp, dom):
        pl.semaphore_signal(barrier, inc=1, device_id=(grp, dom), device_id_type=MESH)

    for a in along:
        greet(line_group(a), j)
    for grp, k, _ in near:
        greet(grp, domain(k))
    for a, k in in_plane:
        greet(plane_group(a), domain(k))

    small = [
        pltpu.make_async_copy(live_hbm, live, small_sem.at[0]),
        pltpu.make_async_copy(halo_hbm, halo, small_sem.at[1]),
        pltpu.make_async_copy(shift_hbm, shift, small_sem.at[2]),
        pltpu.make_async_copy(slot_hbm, slots, small_sem.at[3]),
        pltpu.make_async_copy(count_hbm, count, count_sem),
    ]
    for copy in small[:3]:
        copy.start()
    small[4].start()
    part = blocks // CHUNKS
    big = []
    for c in range(CHUNKS):
        rows = pl.ds(c * part, part)
        big.append([
            pltpu.make_async_copy(mass_hbm.at[rows], mass.at[rows], in_sem.at[3 * c]),
            pltpu.make_async_copy(pos_hbm.at[:, rows], pos.at[:, rows], in_sem.at[3 * c + 1]),
            pltpu.make_async_copy(vel_hbm.at[:, rows], vel.at[:, rows], in_sem.at[3 * c + 2]),
        ])
        for copy in big[-1]:
            copy.start()
    small[3].start()
    for copy in small[:3]:
        copy.wait()
    small[4].wait()

    row = iota((1, blocks), 1)
    live_row = jnp.where(row < count[0], live[...], 0).astype(F32)
    halo_row = halo[...].astype(F32)
    shift_rows = shift[...].astype(F32)
    turned = jnp.concatenate(
        [live_row, halo_row, shift_rows, jnp.zeros((blocks - 5, blocks), F32)], axis=0
    ).T
    live_bc[...] = jnp.broadcast_to(turned[:, 0:1], (blocks, blocks))
    halo_bc[...] = jnp.broadcast_to(turned[:, 1:2], (blocks, blocks))
    for c in range(3):
        shift_bc[c] = jnp.broadcast_to(turned[:, 2 + c : 3 + c], (blocks, blocks))

    tiles = width // 128
    lane = iota((8, 128), 1)
    diagonal = lane - iota((8, 128), 0)

    def moment_step(i, sums):
        base = pl.multiple_of(i * 8, 8)
        rows = pl.ds(base, 8)
        alive = live_bc[rows, :]
        acc = None
        for t in range(tiles):
            cols = pl.ds(t * 128, 128)
            w = jnp.where((lane + t * 128).astype(F32) < alive, mass[rows, cols], 0.0)
            p = [pos[c, rows, cols] for c in range(3)]
            v = [vel[c, rows, cols] for c in range(3)]
            wv = [w * v[c] for c in range(3)]
            terms = [w] + [w * p[c] for c in range(3)] + wv
            terms.append(wv[0] * v[0] + wv[1] * v[1] + wv[2] * v[2])
            terms.append(p[1] * wv[2] - p[2] * wv[1])
            terms.append(p[2] * wv[0] - p[0] * wv[2])
            terms.append(p[0] * wv[1] - p[1] * wv[0])
            acc = terms if acc is None else [a + b for a, b in zip(acc, terms)]
        here = diagonal == base
        return tuple(
            s + jnp.where(here, jnp.sum(a, axis=1, keepdims=True), 0.0)
            for s, a in zip(sums, acc)
        )

    sums = tuple(jnp.zeros((8, 128), F32) for _ in range(11))
    for c in range(CHUNKS):
        for copy in big[c]:
            copy.wait()
        sums = lax.fori_loop(c * part // 8, (c + 1) * part // 8, moment_step, sums, unroll=4)
    m = [jnp.sum(s, axis=0, keepdims=True) for s in sums]
    s = [shift_rows[c : c + 1] for c in range(3)]
    raw_p, mom_v = m[1:4], m[4:7]
    ang = [
        m[8] + (s[1] * mom_v[2] - s[2] * mom_v[1]),
        m[9] + (s[2] * mom_v[0] - s[0] * mom_v[2]),
        m[10] + (s[0] * mom_v[1] - s[1] * mom_v[0]),
    ]
    place = [raw_p[c] + s[c] * m[0] for c in range(3)]

    small[3].wait()
    halo_int = halo[...]
    high_bits = halo_int // 128
    low_bits = halo_int - high_bits * 128
    table = slots[...]
    table_high = table // 256
    table_low = table - table_high * 256
    pick = jnp.where(iota((128, blocks), 0) == low_bits, 1.0, 0.0).astype(jnp.bfloat16)
    picked = jnp.dot(
        jnp.concatenate([table_high, table_low], axis=0).astype(F32).astype(jnp.bfloat16),
        pick,
        preferred_element_type=F32,
    )
    long = table.shape[0]
    both = picked[:long] * 256.0 + picked[long:]
    slot_row = jnp.sum(
        jnp.where(iota((long, blocks), 0) == high_bits, both, 0.0), axis=0, keepdims=True
    )

    message = jnp.concatenate(
        [m[0], *place, *mom_v, m[7], halo_row, slot_row, *ang, jnp.zeros((3, blocks), F32)], axis=0
    )
    moments[...] = message
    extra[...] = m[0]
    me = x * domains + j
    gather[pl.ds(domains + j, 1)] = message[None]
    plane[pl.ds(me, 1)] = m[0][None]

    pl.semaphore_wait(barrier, len(near) + len(in_plane) + len(along))

    for a, k in in_plane:
        pltpu.make_async_remote_copy(
            extra, plane.at[me], send_sem.at[0], recv_sem.at[3],
            device_id=(plane_group(a), domain(k)), device_id_type=MESH,
        ).start()
    for grp, k, d in near:
        pltpu.make_async_remote_copy(
            moments, gather.at[d * domains + j], send_sem.at[1], recv_sem.at[d],
            device_id=(grp, domain(k)), device_id_type=MESH,
        ).start()

    def arrived(d):
        n = domains - 1 if d == 1 else domains
        span = gather.at[pl.ds(d * domains, n)]
        pltpu.make_async_copy(span, span, recv_sem.at[d]).wait()

    def hot(d, base_bc, at):
        return jnp.concatenate(
            [
                jnp.where(base_bc == gather[d * domains + k, at : at + 1, :], 1.0, 0.0).astype(jnp.bfloat16)
                for k in range(domains)
            ],
            axis=1,
        )

    def parts(d, row0, rows):
        values = [
            in_three(gather[d * domains + k, row0 : row0 + rows, :]).astype(jnp.bfloat16)
            for k in range(domains)
        ]
        return jnp.concatenate(values, axis=1)

    def summed(d):
        return lax.dot_general(
            hot(d, halo_bc[...], 8), parts(d, 0, 8), NT, preferred_element_type=F32
        )

    def owned(d):
        mine = (iota((blocks, blocks), 0) + (g * domains + j) * blocks).astype(F32)
        return lax.dot_general(
            hot(d, mine, 9), parts(d, 0, 16), NT, preferred_element_type=F32
        )

    arrived(1)
    stats = summed(1)
    table_sums = owned(1)

    n_plane = len(in_plane)
    pltpu.make_async_copy(plane.at[pl.ds(0, n_plane)], plane.at[pl.ds(0, n_plane)], recv_sem.at[3]).wait()
    plane_mass = jnp.sum(plane[...], axis=0)
    extra_line = plane_mass
    pltpu.make_async_copy(plane.at[pl.ds(0, n_plane)], plane.at[pl.ds(0, n_plane)], send_sem.at[0]).wait()
    extra[...] = extra_line
    line[pl.ds(z, 1)] = plane_mass[None]
    for a in along:
        pltpu.make_async_remote_copy(
            extra, line.at[z], send_sem.at[2], recv_sem.at[4],
            device_id=(line_group(a), j), device_id_type=MESH,
        ).start()

    arrived(0)
    arrived(2)
    stats = stats + summed(0) + summed(2)
    stats = stats[:, 0:8] + stats[:, 8:16] + stats[:, 16:24]
    wide = [jnp.broadcast_to(stats[:, k : k + 1], (blocks, 128)) for k in range(8)]
    heavy = 1.0 / jnp.maximum(wide[0], 1.0)
    drift = [wide[4 + c] * heavy for c in range(3)]
    spread = wide[7] * heavy - (drift[0] * drift[0] + drift[1] * drift[1] + drift[2] * drift[2])
    over = 1.0 / (3.0 * spread + EPSILON)
    centre = [wide[1 + c] * heavy - shift_bc[c] for c in range(3)]

    for i in range(blocks // 8):
        r = slice(8 * i, 8 * i + 8)
        alive = live_bc[r, :]
        for t in range(tiles):
            q = slice(128 * t, 128 * t + 128)
            mask = (lane + t * 128).astype(F32) < alive
            dv = [vel[c, r, q] - drift[c][r] for c in range(3)]
            dp = [pos[c, r, q] - centre[c][r] for c in range(3)]
            kin = (dv[0] * dv[0] + dv[1] * dv[1] + dv[2] * dv[2]) * over[r]
            rad = dp[0] * dp[0] + dp[1] * dp[1] + dp[2] * dp[2]
            kin_ref[r, q] = jnp.where(mask, kin, 0.0)
            rad_ref[r, q] = jnp.where(mask, rad, 0.0)

    table_sums = table_sums + owned(0)
    own = jnp.concatenate([table_sums, jnp.zeros((blocks, 128 - 48), F32)], axis=1).T
    own = own[0:16] + own[16:32] + own[32:48]
    heavy = jnp.maximum(own[0:1], 1.0)
    c = [own[1 + i : 2 + i] / heavy for i in range(3)]
    d = [own[4 + i : 5 + i] / heavy for i in range(3)]
    spread = own[7:8] / heavy - (d[0] * d[0] + d[1] * d[1] + d[2] * d[2])
    spin = [
        own[10:11] / heavy - (c[1] * d[2] - c[2] * d[1]),
        own[11:12] / heavy - (c[2] * d[0] - c[0] * d[2]),
        own[12:13] / heavy - (c[0] * d[1] - c[1] * d[0]),
    ]

    n_line = len(along)
    pltpu.make_async_copy(line.at[pl.ds(0, n_line)], line.at[pl.ds(0, n_line)], recv_sem.at[4]).wait()
    total = jnp.sum(jnp.sum(line[...], axis=0), axis=1, keepdims=True)
    share = own[0:1] * float(groups * domains * blocks) / total
    table_ref[...] = jnp.concatenate([share, *c, *d, spread, *spin], axis=0)

    pltpu.make_async_copy(line.at[pl.ds(0, n_line)], line.at[pl.ds(0, n_line)], send_sem.at[2]).wait()
    n_near = len(near)
    pltpu.make_async_copy(gather.at[pl.ds(0, n_near)], gather.at[pl.ds(0, n_near)], send_sem.at[1]).wait()


def solution(mesh, plane_groups=PLANE_GROUPS):
    groups, domains = mesh.shape["grp"], mesh.shape["dom"]
    both = ("grp", "dom")

    def local(positions, velocities, masses, block_halo, block_shift, block_live, block_count, home_slot):
        blocks, width = masses.shape
        hbm = pl.BlockSpec(memory_space=pltpu.HBM)
        vmem = pl.BlockSpec(memory_space=pltpu.VMEM)
        long = home_slot.shape[0] // 128
        return pl.pallas_call(
            functools.partial(kernel, (groups, domains, plane_groups)),
            out_shape=(
                jax.ShapeDtypeStruct((11, blocks), F32),
                jax.ShapeDtypeStruct((blocks, width), F32),
                jax.ShapeDtypeStruct((blocks, width), F32),
            ),
            in_specs=[hbm] * 8,
            out_specs=(vmem, vmem, vmem),
            scratch_shapes=[
                pltpu.VMEM((3, blocks, width), F32),
                pltpu.VMEM((3, blocks, width), F32),
                pltpu.VMEM((blocks, width), F32),
                pltpu.VMEM((1, blocks), jnp.int32),
                pltpu.VMEM((3, blocks), jnp.int32),
                pltpu.VMEM((1, blocks), jnp.int32),
                pltpu.SMEM((1,), jnp.int32),
                pltpu.VMEM((long, 128), jnp.int32),
                pltpu.VMEM((blocks, blocks), F32),
                pltpu.VMEM((blocks, blocks), F32),
                pltpu.VMEM((3, blocks, blocks), F32),
                pltpu.VMEM((16, blocks), F32),
                pltpu.VMEM((1, blocks), F32),
                pltpu.VMEM((3 * domains, 16, blocks), F32),
                pltpu.VMEM((plane_groups * domains, 1, blocks), F32),
                pltpu.VMEM((groups // plane_groups, 1, blocks), F32),
                pltpu.SemaphoreType.DMA((3 * CHUNKS,)),
                pltpu.SemaphoreType.DMA((4,)),
                pltpu.SemaphoreType.DMA,
                pltpu.SemaphoreType.DMA((3,)),
                pltpu.SemaphoreType.DMA((5,)),
            ],
            compiler_params=pltpu.CompilerParams(collective_id=0, has_side_effects=True),
        )(
            positions, velocities, masses,
            block_halo.reshape(1, blocks), block_shift, block_live.reshape(1, blocks), block_count,
            home_slot.reshape(long, 128),
        )

    return jax.shard_map(
        local,
        mesh=mesh,
        in_specs=(
            P(None, both, None), P(None, both, None), P(both, None), P(both), P(None, both), P(both), P(both), P(),
        ),
        out_specs=(P(None, both), P(both, None), P(both, None)),
        check_vma=False,
    )
```

time: 83 us -> 25.5 us (0.31)
  blocking collectives: 45.6 us -> 0 us
  Pallas kernels: 0 us -> 20.3 us
  starting transfers between devices: 16.9 us -> 0 us
  other arithmetic: 7.06 us -> 0 us
  waiting for transfers between devices: 4.36 us -> 0 us
  local copies, waits for them, and re-layouts: 7.11 us -> 3.72 us
    psum x4 -> x0, blocking collectives: 45.6 us -> none  [over_axes(): return functools.reduce(lax.psum, axes, shard)]
    pallas_call x0 -> x1, Pallas kernels: none -> 20.3 us  [local(): pl.pallas_call(functools.partial(kernel, (groups, domains, plane_groups))...]
    all_to_all x2 -> x0, starting transfers between devices: 11.7 us -> none  [the longest x1 6.47 us: summed_on_arrival(): lax.all_to_all(pieces, axis, split_axis=0, concat_axis=0, tiled=True)]
    ppermute x2 -> x0, starting transfers between devices: 5.18 us -> none  [from_behind(): lax.ppermute(shard, axis, [(i, (i + by) % devices) for i in range(devices)])]
    all_to_all x2 -> x0, waiting for transfers between devices: 3.61 us -> none  [the longest x1 3.61 us: sent_to_all(): lax.all_to_all(jnp.broadcast_to(shard[None], (devices, *shard.shape)), ax...]
    unnamed x15 -> x5, local copies, waits for them, and re-layouts: 1.66 us -> 3.72 us
    gather x2 -> x0, local copies, waits for them, and re-layouts: 1.8 us -> none  [the longest x1 1.15 us: local(): slots = home_slot[block_halo]]
    concatenate x4 -> x0, local copies, waits for them, and re-layouts: 1.72 us -> none  [the longest x1 1.21 us: halo_properties(): jnp.concatenate([share[None], centre, drift, spread[None], spin], axis=0)]
  transfers between devices with their start and end apart: 4 -> 0, of which waited for: 2 -> 0; matrix products, arithmetic and copies ran while one was open for 2% -> 0% of each run, Pallas kernels for 0% -> 0%
where the time goes in v1:
time: 25.5 us; the launch traced here: 25.4 us
  Pallas kernels  20.3 us (80%)
  local copies, waits for them, and re-layouts  3.72 us (15%)
  between operations  1.29 us (5%)
    pallas_call x1, Pallas kernels, local(): pl.pallas_call(functools.partial(kernel, (groups, domains, plane_groups))...  20.3 us
    unnamed x5, local copies, waits for them, and re-layouts  3.72 us

profile of v1, /device:TPU:1, one launch (start us, length us, event | category | flops | bytes accessed | tf_op | source)
XLA Modules:
  0.0 25.4 jit_solution(609283158898311623)
XLA Ops:
  1.3 20.3 %shard_map.103 = (f32[11,128]{1,0:T(8,128)}, f32[128,512]{1,0:T(8,128)}, f32[128,512]{1,0:T(8,128)}) custom-call(f32[3,128,512]{2,1,0:T(8,128)} %pos_hbm.1, f32[3,128,512]{2,1,0:T(8,128)} %vel_hbm.1, f32[128,512]{1,0:T(8,128)} %mass_hbm.1, s32[1,128]{1,0:T(1,128)} %bitcast.4, s32[3,128]{1,0:T(4,128)} %shift_hbm.1, s32[1,128]{1,0:T(1,128)} %bitcast.5, ...), custom_call_target="tpu_custom_call" | custom-call | tf_op jit(solution)/shard_map/pallas_call | solution.py:305
  21.6 1.3 %copy.15 = f32[11,128]{1,0:T(8,128)} copy(f32[11,128]{1,0:T(8,128)} %get-tuple-element.6) | data formatting | bytes 11264
  22.9 0.0 copy-start
  22.9 1.7 %copy.16 = f32[128,512]{1,0:T(8,128)} copy(f32[128,512]{1,0:T(8,128)} %get-tuple-element.7) | data formatting | bytes 524288
  24.6 0.0 copy-done
  24.6 0.7 %copy.17 = f32[128,512]{1,0:T(8,128)} copy(f32[128,512]{1,0:T(8,128)S(1)} %copy-done) | data formatting | bytes 524288
Async XLA Ops:
  22.9 1.7 %copy-start = (f32[128,512]{1,0:T(8,128)S(1)}, f32[128,512]{1,0:T(8,128)}, u32[]{:S(2)}) copy-start(f32[128,512]{1,0:T(8,128)} %get-tuple-element.8) | copy-start | bytes 786436

commit v2 on v1

--- a/solution.py
+++ b/solution.py
@@ -10,6 +10,7 @@
 MESH = pl.DeviceIdType.MESH
 EPSILON = 1e-6
 PLANE_GROUPS = 4
+ROOT_PLANES = 2
 CHUNKS = 2
 F32 = jnp.float32
 NT = (((1,), (1,)), ((), ()))
@@ -35,7 +36,7 @@
     pos_hbm, vel_hbm, mass_hbm, halo_hbm, shift_hbm, live_hbm, count_hbm, slot_hbm,
     table_ref, kin_ref, rad_ref,
     pos, vel, mass, halo, shift, live, count, slots,
-    live_bc, halo_bc, shift_bc, moments, extra, gather, plane, line,
+    live_bc, halo_bc, shift_bc, moments, extra, gather, masses, line,
     in_sem, small_sem, count_sem, send_sem, recv_sem,
 ):
     groups, domains, planes_groups = sizes
@@ -51,40 +52,27 @@
     order = sorted(range(domains), key=lambda k: -min(k, domains - k))
     near = [(grp, k, d) for grp, d in ((nxt, 0), (prv, 2)) for k in order]
     near += [(g, k, 1) for k in order if k]
-    in_plane = [(a, k) for a in range(planes_groups) for k in range(domains) if (a, k) != (0, 0)]
-    along = list(range(1, depth))
+    roots = min(ROOT_PLANES, depth - 1)
+    plane = planes_groups * domains
+    everyone = groups * domains
+    me = g * domains + j
+    is_root = z < roots
 
     def domain(k):
         return wrapped(j + k, domains)
 
-    def plane_group(a):
-        return z * planes_groups + wrapped(x + a, planes_groups)
-
-    def line_group(a):
-        return wrapped(z + a, depth) * planes_groups + x
-
-    barrier = pltpu.get_barrier_semaphore()
-
     def greet(grp, dom):
         pl.semaphore_signal(barrier, inc=1, device_id=(grp, dom), device_id_type=MESH)
 
-    for a in along:
-        greet(line_group(a), j)
-    for grp, k, _ in near:
-        greet(grp, domain(k))
-    for a, k in in_plane:
-        greet(plane_group(a), domain(k))
-
     small = [
         pltpu.make_async_copy(live_hbm, live, small_sem.at[0]),
+        pltpu.make_async_copy(count_hbm, count, count_sem),
         pltpu.make_async_copy(halo_hbm, halo, small_sem.at[1]),
         pltpu.make_async_copy(shift_hbm, shift, small_sem.at[2]),
         pltpu.make_async_copy(slot_hbm, slots, small_sem.at[3]),
-        pltpu.make_async_copy(count_hbm, count, count_sem),
     ]
-    for copy in small[:3]:
+    for copy in small:
         copy.start()
-    small[4].start()
     part = blocks // CHUNKS
     big = []
     for c in range(CHUNKS):
@@ -96,22 +84,50 @@
         ])
         for copy in big[-1]:
             copy.start()
-    small[3].start()
-    for copy in small[:3]:
+
+    barrier = pltpu.get_barrier_semaphore()
+    for grp, k, _ in near:
+        greet(grp, domain(k))
+
+    @pl.when(is_root)
+    def _():
+        @pl.loop(0, groups)
+        def _(step):
+            grp = groups - 1 - step
+            for dom in range(domains):
+                @pl.when((grp != g) | (dom != j))
+                def _():
+                    greet(grp, dom)
+
+    for copy in small:
         copy.wait()
-    small[4].wait()
 
     row = iota((1, blocks), 1)
-    live_row = jnp.where(row < count[0], live[...], 0).astype(F32)
+    live_row = jnp.where(row < count[...], live[...], 0).astype(F32)
     halo_row = halo[...].astype(F32)
     shift_rows = shift[...].astype(F32)
     turned = jnp.concatenate(
         [live_row, halo_row, shift_rows, jnp.zeros((blocks - 5, blocks), F32)], axis=0
     ).T
     live_bc[...] = jnp.broadcast_to(turned[:, 0:1], (blocks, blocks))
-    halo_bc[...] = jnp.broadcast_to(turned[:, 1:2], (blocks, blocks))
-    for c in range(3):
-        shift_bc[c] = jnp.broadcast_to(turned[:, 2 + c : 3 + c], (blocks, blocks))
+
+    halo_int = halo[...]
+    high_bits = halo_int // 128
+    low_bits = halo_int - high_bits * 128
+    table = slots[...]
+    table_high = table // 256
+    table_low = table - table_high * 256
+    pick = jnp.where(iota((128, blocks), 0) == low_bits, 1.0, 0.0).astype(jnp.bfloat16)
+    picked = jnp.dot(
+        jnp.concatenate([table_high, table_low], axis=0).astype(F32).astype(jnp.bfloat16),
+        pick,
+        preferred_element_type=F32,
+    )
+    long = table.shape[0]
+    both = picked[:long] * 256.0 + picked[long:]
+    slot_row = jnp.sum(
+        jnp.where(iota((long, blocks), 0) == high_bits, both, 0.0), axis=0, keepdims=True
+    )
 
     tiles = width // 128
     lane = iota((8, 128), 1)
@@ -155,46 +171,40 @@
     ]
     place = [raw_p[c] + s[c] * m[0] for c in range(3)]
 
-    small[3].wait()
-    halo_int = halo[...]
-    high_bits = halo_int // 128
-    low_bits = halo_int - high_bits * 128
-    table = slots[...]
-    table_high = table // 256
-    table_low = table - table_high * 256
-    pick = jnp.where(iota((128, blocks), 0) == low_bits, 1.0, 0.0).astype(jnp.bfloat16)
-    picked = jnp.dot(
-        jnp.concatenate([table_high, table_low], axis=0).astype(F32).astype(jnp.bfloat16),
-        pick,
-        preferred_element_type=F32,
-    )
-    long = table.shape[0]
-    both = picked[:long] * 256.0 + picked[long:]
-    slot_row = jnp.sum(
-        jnp.where(iota((long, blocks), 0) == high_bits, both, 0.0), axis=0, keepdims=True
-    )
-
     message = jnp.concatenate(
         [m[0], *place, *mom_v, m[7], halo_row, slot_row, *ang, jnp.zeros((3, blocks), F32)], axis=0
     )
     moments[...] = message
     extra[...] = m[0]
-    me = x * domains + j
     gather[pl.ds(domains + j, 1)] = message[None]
-    plane[pl.ds(me, 1)] = m[0][None]
-
-    pl.semaphore_wait(barrier, len(near) + len(in_plane) + len(along))
-
-    for a, k in in_plane:
+    masses[pl.ds(me, 1)] = m[0][None]
+
+    pl.semaphore_wait(barrier, jnp.where(is_root, len(near) + roots * plane - 1, len(near) + roots * plane))
+
+    def send_mass(grp, dom):
         pltpu.make_async_remote_copy(
-            extra, plane.at[me], send_sem.at[0], recv_sem.at[3],
-            device_id=(plane_group(a), domain(k)), device_id_type=MESH,
+            extra, masses.at[me], send_sem.at[0], recv_sem.at[3],
+            device_id=(grp, dom), device_id_type=MESH,
         ).start()
+
+    for r in range(roots):
+        for a in range(planes_groups):
+            for k in order:
+                grp = r * planes_groups + wrapped(x + a, planes_groups)
+                if (a, k) == (0, 0):
+                    @pl.when(z != r)
+                    def _():
+                        send_mass(grp, j)
+                else:
+                    send_mass(grp, domain(k))
     for grp, k, d in near:
         pltpu.make_async_remote_copy(
             moments, gather.at[d * domains + j], send_sem.at[1], recv_sem.at[d],
             device_id=(grp, domain(k)), device_id_type=MESH,
         ).start()
+    halo_bc[...] = jnp.broadcast_to(turned[:, 1:2], (blocks, blocks))
+    for c in range(3):
+        shift_bc[c] = jnp.broadcast_to(turned[:, 2 + c : 3 + c], (blocks, blocks))
 
     def arrived(d):
         n = domains - 1 if d == 1 else domains
@@ -225,29 +235,17 @@
     def owned(d):
         mine = (iota((blocks, blocks), 0) + (g * domains + j) * blocks).astype(F32)
         return lax.dot_general(
-            hot(d, mine, 9), parts(d, 0, 16), NT, preferred_element_type=F32
+            parts(d, 0, 16), hot(d, mine, 9), NT, preferred_element_type=F32
         )
 
     arrived(1)
     stats = summed(1)
     table_sums = owned(1)
 
-    n_plane = len(in_plane)
-    pltpu.make_async_copy(plane.at[pl.ds(0, n_plane)], plane.at[pl.ds(0, n_plane)], recv_sem.at[3]).wait()
-    plane_mass = jnp.sum(plane[...], axis=0)
-    extra_line = plane_mass
-    pltpu.make_async_copy(plane.at[pl.ds(0, n_plane)], plane.at[pl.ds(0, n_plane)], send_sem.at[0]).wait()
-    extra[...] = extra_line
-    line[pl.ds(z, 1)] = plane_mass[None]
-    for a in along:
-        pltpu.make_async_remote_copy(
-            extra, line.at[z], send_sem.at[2], recv_sem.at[4],
-            device_id=(line_group(a), j), device_id_type=MESH,
-        ).start()
-
+    arrived(2)
+    stats = stats + summed(2)
     arrived(0)
-    arrived(2)
-    stats = stats + summed(0) + summed(2)
+    stats = stats + summed(0)
     stats = stats[:, 0:8] + stats[:, 8:16] + stats[:, 16:24]
     wide = [jnp.broadcast_to(stats[:, k : k + 1], (blocks, 128)) for k in range(8)]
     heavy = 1.0 / jnp.maximum(wide[0], 1.0)
@@ -270,8 +268,7 @@
             rad_ref[r, q] = jnp.where(mask, rad, 0.0)
 
     table_sums = table_sums + owned(0)
-    own = jnp.concatenate([table_sums, jnp.zeros((blocks, 128 - 48), F32)], axis=1).T
-    own = own[0:16] + own[16:32] + own[32:48]
+    own = table_sums[0:16] + table_sums[16:32] + table_sums[32:48]
     heavy = jnp.maximum(own[0:1], 1.0)
     c = [own[1 + i : 2 + i] / heavy for i in range(3)]
     d = [own[4 + i : 5 + i] / heavy for i in range(3)]
@@ -282,15 +279,63 @@
         own[12:13] / heavy - (c[0] * d[1] - c[1] * d[0]),
     ]
 
-    n_line = len(along)
-    pltpu.make_async_copy(line.at[pl.ds(0, n_line)], line.at[pl.ds(0, n_line)], recv_sem.at[4]).wait()
-    total = jnp.sum(jnp.sum(line[...], axis=0), axis=1, keepdims=True)
+    def along(r):
+        return [t for t in range(roots, depth) if (t > depth // 2) == (r == 0)] if roots > 1 else list(range(roots, depth))
+
+    def tell(t):
+        return pltpu.make_async_remote_copy(
+            line, line, send_sem.at[2], recv_sem.at[4],
+            device_id=(t * planes_groups + x, j), device_id_type=MESH,
+        )
+
+    @pl.when(is_root)
+    def _():
+        others = masses.at[pl.ds(0, everyone - 1)]
+        pltpu.make_async_copy(others, others, recv_sem.at[3]).wait()
+        line[...] = jnp.sum(masses[...], axis=0)
+        for r in (0, roots - 1)[: min(roots, 2)]:
+            @pl.when(z == r)
+            def _():
+                for t in along(r):
+                    tell(t).start()
+
+    @pl.when(z >= roots)
+    def _():
+        pltpu.make_async_copy(line, line, recv_sem.at[4]).wait()
+
+    total = jnp.sum(line[...], axis=1, keepdims=True)
     share = own[0:1] * float(groups * domains * blocks) / total
     table_ref[...] = jnp.concatenate([share, *c, *d, spread, *spin], axis=0)
 
-    pltpu.make_async_copy(line.at[pl.ds(0, n_line)], line.at[pl.ds(0, n_line)], send_sem.at[2]).wait()
+    for r in (0, roots - 1)[: min(roots, 2)]:
+        @pl.when(z == r)
+        def _():
+            told = masses.at[pl.ds(0, len(along(r)))]
+            pltpu.make_async_copy(told, told, send_sem.at[2]).wait()
+
+    n_mass = roots * plane
+
+    @pl.when(is_root)
+    def _():
+        sent = masses.at[pl.ds(0, n_mass - 1)]
+        pltpu.make_async_copy(sent, sent, send_sem.at[0]).wait()
+
+    @pl.when(z >= roots)
+    def _():
+        sent = masses.at[pl.ds(0, n_mass)]
+        pltpu.make_async_copy(sent, sent, send_sem.at[0]).wait()
+
     n_near = len(near)
     pltpu.make_async_copy(gather.at[pl.ds(0, n_near)], gather.at[pl.ds(0, n_near)], send_sem.at[1]).wait()
+
+
+def flush(table_ref, kin_ref, rad_ref, table_hbm, kin_hbm, rad_hbm, sem):
+    pairs = ((kin_ref, kin_hbm), (rad_ref, rad_hbm), (table_ref, table_hbm))
+    copies = [pltpu.make_async_copy(a, b, sem.at[i]) for i, (a, b) in enumerate(pairs)]
+    for copy in copies:
+        copy.start()
+    for copy in copies:
+        copy.wait()
 
 
 def solution(mesh, plane_groups=PLANE_GROUPS):
@@ -302,12 +347,12 @@
         hbm = pl.BlockSpec(memory_space=pltpu.HBM)
         vmem = pl.BlockSpec(memory_space=pltpu.VMEM)
         long = home_slot.shape[0] // 128
-        return pl.pallas_call(
+        results = pl.pallas_call(
             functools.partial(kernel, (groups, domains, plane_groups)),
             out_shape=(
-                jax.ShapeDtypeStruct((11, blocks), F32),
-                jax.ShapeDtypeStruct((blocks, width), F32),
-                jax.ShapeDtypeStruct((blocks, width), F32),
+                pltpu.VMEM((11, blocks), F32),
+                pltpu.VMEM((blocks, width), F32),
+                pltpu.VMEM((blocks, width), F32),
             ),
             in_specs=[hbm] * 8,
             out_specs=(vmem, vmem, vmem),
@@ -318,7 +363,7 @@
                 pltpu.VMEM((1, blocks), jnp.int32),
                 pltpu.VMEM((3, blocks), jnp.int32),
                 pltpu.VMEM((1, blocks), jnp.int32),
-                pltpu.SMEM((1,), jnp.int32),
+                pltpu.VMEM((1, 1), jnp.int32),
                 pltpu.VMEM((long, 128), jnp.int32),
                 pltpu.VMEM((blocks, blocks), F32),
                 pltpu.VMEM((blocks, blocks), F32),
@@ -326,8 +371,8 @@
                 pltpu.VMEM((16, blocks), F32),
                 pltpu.VMEM((1, blocks), F32),
                 pltpu.VMEM((3 * domains, 16, blocks), F32),
-                pltpu.VMEM((plane_groups * domains, 1, blocks), F32),
-                pltpu.VMEM((groups // plane_groups, 1, blocks), F32),
+                pltpu.VMEM((groups * domains, 1, blocks), F32),
+                pltpu.VMEM((1, blocks), F32),
                 pltpu.SemaphoreType.DMA((3 * CHUNKS,)),
                 pltpu.SemaphoreType.DMA((4,)),
                 pltpu.SemaphoreType.DMA,
@@ -337,9 +382,16 @@
             compiler_params=pltpu.CompilerParams(collective_id=0, has_side_effects=True),
         )(
             positions, velocities, masses,
-            block_halo.reshape(1, blocks), block_shift, block_live.reshape(1, blocks), block_count,
+            block_halo.reshape(1, blocks), block_shift, block_live.reshape(1, blocks), block_count.reshape(1, 1),
             home_slot.reshape(long, 128),
         )
+        return pl.pallas_call(
+            flush,
+            out_shape=tuple(jax.ShapeDtypeStruct(r.shape, F32) for r in results),
+            in_specs=[vmem] * 3,
+            out_specs=(hbm,) * 3,
+            scratch_shapes=[pltpu.SemaphoreType.DMA((3,))],
+        )(*[pltpu.with_memory_space_constraint(r, pltpu.VMEM) for r in results])
 
     return jax.shard_map(
         local,

time: 25.5 us -> 21.8 us (0.85)
  local copies, waits for them, and re-layouts: 3.72 us -> 0 us
    unnamed x5 -> x0, local copies, waits for them, and re-layouts: 3.72 us -> none
    pallas_call x0 -> x1, Pallas kernels: none -> 0.82 us  [local(): pl.pallas_call(flush, out_shape=tuple((jax.ShapeDtypeStruct(r.shape, F32)...]
    pallas_call x1, Pallas kernels: 20.3 us -> 19.6 us  [local(): pl.pallas_call(functools.partial(kernel, (groups, domains, plane_groups))...]
where the time goes in v2:
time: 21.8 us; the launch traced here: 21.7 us
  Pallas kernels  20.4 us (94%)
  between operations  1.29 us (6%)
    pallas_call x1, Pallas kernels, local(): pl.pallas_call(functools.partial(kernel, (groups, domains, plane_groups))...  19.6 us
    pallas_call x1, Pallas kernels, local(): pl.pallas_call(flush, out_shape=tuple((jax.ShapeDtypeStruct(r.shape, F32)...  0.82 us

profile of v2, /device:TPU:1, one launch (start us, length us, event | category | flops | bytes accessed | tf_op | source)
XLA Modules:
  0.0 21.7 jit_solution(3193492374623387868)
XLA Ops:
  1.3 19.6 %shard_map.103 = (f32[11,128]{1,0:T(8,128)S(1)}, f32[128,512]{1,0:T(8,128)S(1)}, f32[128,512]{1,0:T(8,128)S(1)}) custom-call(f32[3,128,512]{2,1,0:T(8,128)} %pos_hbm.1, f32[3,128,512]{2,1,0:T(8,128)} %vel_hbm.1, f32[128,512]{1,0:T(8,128)} %mass_hbm.1, s32[1,128]{1,0:T(1,128)} %bitcast.6, s32[3,128]{1,0:T(4,128)} %shift_hbm.1, s32[1,128]{1,0:T(1,128)} %bitcast.7, ...), custom_call_target="tpu_custom_call" | custom-call | tf_op jit(solution)/shard_map/pallas_call | solution.py:350
  20.9 0.8 %shard_map.104 = (f32[11,128]{1,0:T(8,128)}, f32[128,512]{1,0:T(8,128)}, f32[128,512]{1,0:T(8,128)}) custom-call(f32[11,128]{1,0:T(8,128)S(1)} %get-tuple-element.6.table_ref, f32[128,512]{1,0:T(8,128)S(1)} %get-tuple-element.7.kin_ref, f32[128,512]{1,0:T(8,128)S(1)} %get-tuple-element.8.rad_ref), custom_call_target="tpu_custom_call" | custom-call | tf_op jit(solution)/shard_map/pallas_call | solution.py:388

commit v3 on v2

--- a/solution.py
+++ b/solution.py
@@ -10,8 +10,8 @@
 MESH = pl.DeviceIdType.MESH
 EPSILON = 1e-6
 PLANE_GROUPS = 4
-ROOT_PLANES = 2
-CHUNKS = 2
+ROOT = 1
+CHUNKS = 4
 F32 = jnp.float32
 NT = (((1,), (1,)), ((), ()))
 
@@ -36,7 +36,7 @@
     pos_hbm, vel_hbm, mass_hbm, halo_hbm, shift_hbm, live_hbm, count_hbm, slot_hbm,
     table_ref, kin_ref, rad_ref,
     pos, vel, mass, halo, shift, live, count, slots,
-    live_bc, halo_bc, shift_bc, moments, extra, gather, masses, line,
+    live_bc, halo_bc, shift_bc, moments, rest, gather, gather_rest, masses, line,
     in_sem, small_sem, count_sem, send_sem, recv_sem,
 ):
     groups, domains, planes_groups = sizes
@@ -50,13 +50,11 @@
     prv = jnp.where(g == 0, groups - 1, g - 1)
 
     order = sorted(range(domains), key=lambda k: -min(k, domains - k))
-    near = [(grp, k, d) for grp, d in ((nxt, 0), (prv, 2)) for k in order]
-    near += [(g, k, 1) for k in order if k]
-    roots = min(ROOT_PLANES, depth - 1)
-    plane = planes_groups * domains
+    near = [(nxt, k, 0) for k in order] + [(prv, k, 2) for k in order] + [(g, k, 1) for k in order if k]
+    me = g * domains + j
+    roots = depth // 2
     everyone = groups * domains
-    me = g * domains + j
-    is_root = z < roots
+    is_root = (z < roots) & (x == 0) & (j == ROOT)
 
     def domain(k):
         return wrapped(j + k, domains)
@@ -71,7 +69,7 @@
         pltpu.make_async_copy(shift_hbm, shift, small_sem.at[2]),
         pltpu.make_async_copy(slot_hbm, slots, small_sem.at[3]),
     ]
-    for copy in small:
+    for copy in small[:2]:
         copy.start()
     part = blocks // CHUNKS
     big = []
@@ -85,49 +83,32 @@
         for copy in big[-1]:
             copy.start()
 
+    for copy in small[2:]:
+        copy.start()
     barrier = pltpu.get_barrier_semaphore()
     for grp, k, _ in near:
         greet(grp, domain(k))
 
     @pl.when(is_root)
     def _():
-        @pl.loop(0, groups)
+        @pl.loop(0, depth)
         def _(step):
-            grp = groups - 1 - step
-            for dom in range(domains):
-                @pl.when((grp != g) | (dom != j))
-                def _():
-                    greet(grp, dom)
-
-    for copy in small:
+            there = depth - 1 - step
+            for a in range(planes_groups):
+                for k in range(domains):
+                    if (a, k) != (0, ROOT):
+                        greet(there * planes_groups + a, k)
+
+            @pl.when(there != z)
+            def _():
+                greet(there * planes_groups, ROOT)
+
+    for copy in small[:2]:
         copy.wait()
 
     row = iota((1, blocks), 1)
     live_row = jnp.where(row < count[...], live[...], 0).astype(F32)
-    halo_row = halo[...].astype(F32)
-    shift_rows = shift[...].astype(F32)
-    turned = jnp.concatenate(
-        [live_row, halo_row, shift_rows, jnp.zeros((blocks - 5, blocks), F32)], axis=0
-    ).T
-    live_bc[...] = jnp.broadcast_to(turned[:, 0:1], (blocks, blocks))
-
-    halo_int = halo[...]
-    high_bits = halo_int // 128
-    low_bits = halo_int - high_bits * 128
-    table = slots[...]
-    table_high = table // 256
-    table_low = table - table_high * 256
-    pick = jnp.where(iota((128, blocks), 0) == low_bits, 1.0, 0.0).astype(jnp.bfloat16)
-    picked = jnp.dot(
-        jnp.concatenate([table_high, table_low], axis=0).astype(F32).astype(jnp.bfloat16),
-        pick,
-        preferred_element_type=F32,
-    )
-    long = table.shape[0]
-    both = picked[:long] * 256.0 + picked[long:]
-    slot_row = jnp.sum(
-        jnp.where(iota((long, blocks), 0) == high_bits, both, 0.0), axis=0, keepdims=True
-    )
+    live_bc[...] = jnp.broadcast_to(live_row, (blocks, blocks)).T
 
     tiles = width // 128
     lane = iota((8, 128), 1)
@@ -161,6 +142,10 @@
         for copy in big[c]:
             copy.wait()
         sums = lax.fori_loop(c * part // 8, (c + 1) * part // 8, moment_step, sums, unroll=4)
+    for copy in small[2:]:
+        copy.wait()
+    halo_row = halo[...].astype(F32)
+    shift_rows = shift[...].astype(F32)
     m = [jnp.sum(s, axis=0, keepdims=True) for s in sums]
     s = [shift_rows[c : c + 1] for c in range(3)]
     raw_p, mom_v = m[1:4], m[4:7]
@@ -171,81 +156,99 @@
     ]
     place = [raw_p[c] + s[c] * m[0] for c in range(3)]
 
-    message = jnp.concatenate(
-        [m[0], *place, *mom_v, m[7], halo_row, slot_row, *ang, jnp.zeros((3, blocks), F32)], axis=0
-    )
-    moments[...] = message
-    extra[...] = m[0]
-    gather[pl.ds(domains + j, 1)] = message[None]
-    masses[pl.ds(me, 1)] = m[0][None]
-
-    pl.semaphore_wait(barrier, jnp.where(is_root, len(near) + roots * plane - 1, len(near) + roots * plane))
-
-    def send_mass(grp, dom):
-        pltpu.make_async_remote_copy(
-            extra, masses.at[me], send_sem.at[0], recv_sem.at[3],
-            device_id=(grp, dom), device_id_type=MESH,
-        ).start()
+    moments[0:9, :] = jnp.concatenate([m[0], *place, *mom_v, m[7], halo_row], axis=0)
+    gather[domains + j, 0:9, :] = moments[0:9, :]
+    masses[pl.ds(me, 1), :] = m[0]
+
+    pl.semaphore_wait(barrier, jnp.where(is_root, len(near) + roots - 1, len(near) + roots))
 
     for r in range(roots):
-        for a in range(planes_groups):
-            for k in order:
-                grp = r * planes_groups + wrapped(x + a, planes_groups)
-                if (a, k) == (0, 0):
-                    @pl.when(z != r)
-                    def _():
-                        send_mass(grp, j)
-                else:
-                    send_mass(grp, domain(k))
+        @pl.when(jnp.logical_not(is_root & (z == r)))
+        def _():
+            pltpu.make_async_remote_copy(
+                moments.at[pl.ds(0, 1)], masses.at[pl.ds(me, 1)], send_sem.at[0], recv_sem.at[3],
+                device_id=(r * planes_groups, ROOT), device_id_type=MESH,
+            ).start()
+
     for grp, k, d in near:
         pltpu.make_async_remote_copy(
-            moments, gather.at[d * domains + j], send_sem.at[1], recv_sem.at[d],
+            moments.at[pl.ds(0, 9)], gather.at[d * domains + j, pl.ds(0, 9)], send_sem.at[1], recv_sem.at[d],
             device_id=(grp, domain(k)), device_id_type=MESH,
         ).start()
-    halo_bc[...] = jnp.broadcast_to(turned[:, 1:2], (blocks, blocks))
+    halo_int = halo[...]
+    high_bits = halo_int // 128
+    low_bits = halo_int - high_bits * 128
+    table = slots[...]
+    table_high = table // 256
+    table_low = table - table_high * 256
+    pick = jnp.where(iota((128, blocks), 0) == low_bits, 1.0, 0.0).astype(jnp.bfloat16)
+    picked = jnp.dot(
+        jnp.concatenate([table_high, table_low], axis=0).astype(F32).astype(jnp.bfloat16),
+        pick,
+        preferred_element_type=F32,
+    )
+    long = table.shape[0]
+    both = picked[:long] * 256.0 + picked[long:]
+    slot_row = jnp.sum(
+        jnp.where(iota((long, blocks), 0) == high_bits, both, 0.0), axis=0, keepdims=True
+    )
+
+    rest[0:4, :] = jnp.concatenate([slot_row, *ang], axis=0)
+    gather_rest[domains + j, 0:4, :] = rest[0:4, :]
+    for grp, k, d in near:
+        if d < 2:
+            pltpu.make_async_remote_copy(
+                rest.at[pl.ds(0, 4)], gather_rest.at[d * domains + j, pl.ds(0, 4)], send_sem.at[3], recv_sem.at[5 + d],
+                device_id=(grp, domain(k)), device_id_type=MESH,
+            ).start()
+    halo_bc[...] = jnp.broadcast_to(halo_row, (blocks, blocks)).T
     for c in range(3):
-        shift_bc[c] = jnp.broadcast_to(turned[:, 2 + c : 3 + c], (blocks, blocks))
+        shift_bc[c] = jnp.broadcast_to(s[c], (blocks, blocks)).T
 
     def arrived(d):
         n = domains - 1 if d == 1 else domains
-        span = gather.at[pl.ds(d * domains, n)]
+        span = gather.at[pl.ds(d * domains, n), pl.ds(0, 9)]
         pltpu.make_async_copy(span, span, recv_sem.at[d]).wait()
 
-    def hot(d, base_bc, at):
+    def rest_arrived(d):
+        n = domains - 1 if d == 1 else domains
+        span = gather_rest.at[pl.ds(d * domains, n), pl.ds(0, 4)]
+        pltpu.make_async_copy(span, span, recv_sem.at[5 + d]).wait()
+
+    def hot(values, row):
         return jnp.concatenate(
-            [
-                jnp.where(base_bc == gather[d * domains + k, at : at + 1, :], 1.0, 0.0).astype(jnp.bfloat16)
-                for k in range(domains)
-            ],
-            axis=1,
-        )
-
-    def parts(d, row0, rows):
-        values = [
-            in_three(gather[d * domains + k, row0 : row0 + rows, :]).astype(jnp.bfloat16)
-            for k in range(domains)
-        ]
-        return jnp.concatenate(values, axis=1)
+            [jnp.where(values == r, 1.0, 0.0).astype(jnp.bfloat16) for r in row], axis=1
+        )
+
+    def parts(values):
+        return jnp.concatenate([in_three(v).astype(jnp.bfloat16) for v in values], axis=1)
+
+    def slot_of(d):
+        return [d * domains + k for k in range(domains)]
 
     def summed(d):
         return lax.dot_general(
-            hot(d, halo_bc[...], 8), parts(d, 0, 8), NT, preferred_element_type=F32
+            hot(halo_bc[...], [gather[q, 8:9, :] for q in slot_of(d)]),
+            parts([gather[q, 0:8, :] for q in slot_of(d)]),
+            NT, preferred_element_type=F32,
         )
 
     def owned(d):
-        mine = (iota((blocks, blocks), 0) + (g * domains + j) * blocks).astype(F32)
+        mine = (iota((blocks, blocks), 0) + me * blocks).astype(F32)
+        values = [
+            jnp.concatenate([gather[q, 0:8, :], gather_rest[q, 0:8, :]], axis=0) for q in slot_of(d)
+        ]
         return lax.dot_general(
-            parts(d, 0, 16), hot(d, mine, 9), NT, preferred_element_type=F32
-        )
-
-    arrived(1)
-    stats = summed(1)
-    table_sums = owned(1)
+            parts(values), hot(mine, [gather_rest[q, 0:1, :] for q in slot_of(d)]),
+            NT, preferred_element_type=F32,
+        )
 
     arrived(2)
-    stats = stats + summed(2)
+    stats = summed(2)
     arrived(0)
     stats = stats + summed(0)
+    arrived(1)
+    stats = stats + summed(1)
     stats = stats[:, 0:8] + stats[:, 8:16] + stats[:, 16:24]
     wide = [jnp.broadcast_to(stats[:, k : k + 1], (blocks, 128)) for k in range(8)]
     heavy = 1.0 / jnp.maximum(wide[0], 1.0)
@@ -267,39 +270,49 @@
             kin_ref[r, q] = jnp.where(mask, kin, 0.0)
             rad_ref[r, q] = jnp.where(mask, rad, 0.0)
 
-    table_sums = table_sums + owned(0)
+    rest_arrived(1)
+    rest_arrived(0)
+    table_sums = owned(1) + owned(0)
     own = table_sums[0:16] + table_sums[16:32] + table_sums[32:48]
     heavy = jnp.maximum(own[0:1], 1.0)
     c = [own[1 + i : 2 + i] / heavy for i in range(3)]
     d = [own[4 + i : 5 + i] / heavy for i in range(3)]
     spread = own[7:8] / heavy - (d[0] * d[0] + d[1] * d[1] + d[2] * d[2])
     spin = [
-        own[10:11] / heavy - (c[1] * d[2] - c[2] * d[1]),
-        own[11:12] / heavy - (c[2] * d[0] - c[0] * d[2]),
-        own[12:13] / heavy - (c[0] * d[1] - c[1] * d[0]),
+        own[9:10] / heavy - (c[1] * d[2] - c[2] * d[1]),
+        own[10:11] / heavy - (c[2] * d[0] - c[0] * d[2]),
+        own[11:12] / heavy - (c[0] * d[1] - c[1] * d[0]),
     ]
 
-    def along(r):
-        return [t for t in range(roots, depth) if (t > depth // 2) == (r == 0)] if roots > 1 else list(range(roots, depth))
-
-    def tell(t):
+    def served(r):
+        share = min(2, roots)
+        return [p for p in range(roots, depth) if roots - 1 - (p - roots) * share // (depth - roots) == r]
+
+    def tell(there, a, k):
         return pltpu.make_async_remote_copy(
             line, line, send_sem.at[2], recv_sem.at[4],
-            device_id=(t * planes_groups + x, j), device_id_type=MESH,
+            device_id=(there * planes_groups + a, k), device_id_type=MESH,
         )
 
     @pl.when(is_root)
     def _():
         others = masses.at[pl.ds(0, everyone - 1)]
         pltpu.make_async_copy(others, others, recv_sem.at[3]).wait()
-        line[...] = jnp.sum(masses[...], axis=0)
-        for r in (0, roots - 1)[: min(roots, 2)]:
+        rows = masses[...].reshape(everyone // 8, 8, blocks)
+        line[...] = jnp.sum(jnp.sum(rows, axis=0), axis=0, keepdims=True)
+        for a in range(planes_groups):
+            for k in range(domains):
+                if (a, k) != (0, ROOT):
+                    tell(z, a, k).start()
+        for r in range(roots):
             @pl.when(z == r)
             def _():
-                for t in along(r):
-                    tell(t).start()
-
-    @pl.when(z >= roots)
+                for there in served(r):
+                    for a in range(planes_groups):
+                        for k in range(domains):
+                            tell(there, a, k).start()
+
+    @pl.when(jnp.logical_not(is_root))
     def _():
         pltpu.make_async_copy(line, line, recv_sem.at[4]).wait()
 
@@ -307,26 +320,27 @@
     share = own[0:1] * float(groups * domains * blocks) / total
     table_ref[...] = jnp.concatenate([share, *c, *d, spread, *spin], axis=0)
 
-    for r in (0, roots - 1)[: min(roots, 2)]:
-        @pl.when(z == r)
-        def _():
-            told = masses.at[pl.ds(0, len(along(r)))]
-            pltpu.make_async_copy(told, told, send_sem.at[2]).wait()
-
-    n_mass = roots * plane
-
     @pl.when(is_root)
     def _():
-        sent = masses.at[pl.ds(0, n_mass - 1)]
+        for r in range(roots):
+            @pl.when(z == r)
+            def _():
+                told = masses.at[pl.ds(0, (1 + len(served(r))) * planes_groups * domains - 1)]
+                pltpu.make_async_copy(told, told, send_sem.at[2]).wait()
+
+        sent = masses.at[pl.ds(0, roots - 1)]
         pltpu.make_async_copy(sent, sent, send_sem.at[0]).wait()
 
-    @pl.when(z >= roots)
+    @pl.when(jnp.logical_not(is_root))
     def _():
-        sent = masses.at[pl.ds(0, n_mass)]
+        sent = masses.at[pl.ds(0, roots)]
         pltpu.make_async_copy(sent, sent, send_sem.at[0]).wait()
 
     n_near = len(near)
-    pltpu.make_async_copy(gather.at[pl.ds(0, n_near)], gather.at[pl.ds(0, n_near)], send_sem.at[1]).wait()
+    sent = gather.at[pl.ds(0, n_near), pl.ds(0, 9)]
+    pltpu.make_async_copy(sent, sent, send_sem.at[1]).wait()
+    sent = gather_rest.at[pl.ds(0, 2 * domains - 1), pl.ds(0, 4)]
+    pltpu.make_async_copy(sent, sent, send_sem.at[3]).wait()
 
 
 def flush(table_ref, kin_ref, rad_ref, table_hbm, kin_hbm, rad_hbm, sem):
@@ -369,15 +383,16 @@
                 pltpu.VMEM((blocks, blocks), F32),
                 pltpu.VMEM((3, blocks, blocks), F32),
                 pltpu.VMEM((16, blocks), F32),
-                pltpu.VMEM((1, blocks), F32),
+                pltpu.VMEM((8, blocks), F32),
                 pltpu.VMEM((3 * domains, 16, blocks), F32),
-                pltpu.VMEM((groups * domains, 1, blocks), F32),
+                pltpu.VMEM((2 * domains, 8, blocks), F32),
+                pltpu.VMEM((groups * domains, blocks), F32),
                 pltpu.VMEM((1, blocks), F32),
                 pltpu.SemaphoreType.DMA((3 * CHUNKS,)),
                 pltpu.SemaphoreType.DMA((4,)),
                 pltpu.SemaphoreType.DMA,
-                pltpu.SemaphoreType.DMA((3,)),
-                pltpu.SemaphoreType.DMA((5,)),
+                pltpu.SemaphoreType.DMA((4,)),
+                pltpu.SemaphoreType.DMA((7,)),
             ],
             compiler_params=pltpu.CompilerParams(collective_id=0, has_side_effects=True),
         )(

time: 21.8 us -> 20.3 us (0.931)
  Pallas kernels: 20.4 us -> 18.9 us
    pallas_call x1, Pallas kernels: 19.6 us -> 18.1 us  [local(): pl.pallas_call(functools.partial(kernel, (groups, domains, plane_groups))...]
where the time goes in v3:
time: 20.3 us; the launch traced here: 20.2 us
  Pallas kernels  18.9 us (93%)
  between operations  1.29 us (6%)
    pallas_call x1, Pallas kernels, local(): pl.pallas_call(functools.partial(kernel, (groups, domains, plane_groups))...  18.1 us
    pallas_call x1, Pallas kernels, local(): pl.pallas_call(flush, out_shape=tuple((jax.ShapeDtypeStruct(r.shape, F32)...  0.82 us

profile of v3, /device:TPU:1, one launch (start us, length us, event | category | flops | bytes accessed | tf_op | source)
XLA Modules:
  0.0 20.2 jit_solution(7554236116610930982)
XLA Ops:
  1.3 18.1 %shard_map.103 = (f32[11,128]{1,0:T(8,128)S(1)}, f32[128,512]{1,0:T(8,128)S(1)}, f32[128,512]{1,0:T(8,128)S(1)}) custom-call(f32[3,128,512]{2,1,0:T(8,128)} %pos_hbm.1, f32[3,128,512]{2,1,0:T(8,128)} %vel_hbm.1, f32[128,512]{1,0:T(8,128)} %mass_hbm.1, s32[1,128]{1,0:T(1,128)} %bitcast.6, s32[3,128]{1,0:T(4,128)} %shift_hbm.1, s32[1,128]{1,0:T(1,128)} %bitcast.7, ...), custom_call_target="tpu_custom_call" | custom-call | tf_op jit(solution)/shard_map/pallas_call | solution.py:364
  19.4 0.8 %shard_map.104 = (f32[11,128]{1,0:T(8,128)}, f32[128,512]{1,0:T(8,128)}, f32[128,512]{1,0:T(8,128)}) custom-call(f32[11,128]{1,0:T(8,128)S(1)} %get-tuple-element.6.table_ref, f32[128,512]{1,0:T(8,128)S(1)} %get-tuple-element.7.kin_ref, f32[128,512]{1,0:T(8,128)S(1)} %get-tuple-element.8.rad_ref), custom_call_target="tpu_custom_call" | custom-call | tf_op jit(solution)/shard_map/pallas_call | solution.py:403

commit v4 on v3

--- a/solution.py
+++ b/solution.py
@@ -29,6 +29,19 @@
     rest = x - high
     middle = rest.astype(jnp.bfloat16).astype(F32)
     return jnp.concatenate([high, middle, rest - middle], axis=0)
+
+
+def roots_of(depth, planes_groups, domains):
+    half = depth // 2
+    second = (ROOT + 2) % domains if domains > 2 else 0
+    plane = [(a, k) for a in range(planes_groups) for k in range(domains)]
+    tree = [((0, 0, ROOT), []), ((0, 0, second), [(0, 0, k) for k in range(domains) if k not in (ROOT, second)])]
+    tree += [((0, a, ROOT), [(0, a, k) for k in range(domains) if k != ROOT]) for a in range(1, planes_groups)]
+    share = max(1, min(2, half - 1))
+    for r in range(1, half):
+        late = [p for p in range(half, depth) if half - 1 - (p - half) * share // (depth - half) == r]
+        tree.append(((r, 0, ROOT), [(p, a, k) for p in [r] + late for a, k in plane if (p, a, k) != (r, 0, ROOT)]))
+    return tree
 
 
 def kernel(
@@ -52,9 +65,11 @@
     order = sorted(range(domains), key=lambda k: -min(k, domains - k))
     near = [(nxt, k, 0) for k in order] + [(prv, k, 2) for k in order] + [(g, k, 1) for k in order if k]
     me = g * domains + j
-    roots = depth // 2
     everyone = groups * domains
-    is_root = (z < roots) & (x == 0) & (j == ROOT)
+    tree = roots_of(depth, planes_groups, domains)
+    n_roots = len(tree)
+    i_am = [(g == there * planes_groups + a) & (j == k) for (there, a, k), _ in tree]
+    is_root = functools.reduce(jnp.logical_or, i_am)
 
     def domain(k):
         return wrapped(j + k, domains)
@@ -96,12 +111,12 @@
             there = depth - 1 - step
             for a in range(planes_groups):
                 for k in range(domains):
-                    if (a, k) != (0, ROOT):
+                    if (a, k) in {root[1:] for root, _ in tree}:
+                        @pl.when((there * planes_groups + a != g) | (j != k))
+                        def _():
+                            greet(there * planes_groups + a, k)
+                    else:
                         greet(there * planes_groups + a, k)
-
-            @pl.when(there != z)
-            def _():
-                greet(there * planes_groups, ROOT)
 
     for copy in small[:2]:
         copy.wait()
@@ -160,14 +175,14 @@
     gather[domains + j, 0:9, :] = moments[0:9, :]
     masses[pl.ds(me, 1), :] = m[0]
 
-    pl.semaphore_wait(barrier, jnp.where(is_root, len(near) + roots - 1, len(near) + roots))
-
-    for r in range(roots):
-        @pl.when(jnp.logical_not(is_root & (z == r)))
+    pl.semaphore_wait(barrier, jnp.where(is_root, len(near) + n_roots - 1, len(near) + n_roots))
+
+    for mine, ((there, a, k), _) in zip(i_am, tree):
+        @pl.when(jnp.logical_not(mine))
         def _():
             pltpu.make_async_remote_copy(
                 moments.at[pl.ds(0, 1)], masses.at[pl.ds(me, 1)], send_sem.at[0], recv_sem.at[3],
-                device_id=(r * planes_groups, ROOT), device_id_type=MESH,
+                device_id=(there * planes_groups + a, k), device_id_type=MESH,
             ).start()
 
     for grp, k, d in near:
@@ -247,6 +262,8 @@
     stats = summed(2)
     arrived(0)
     stats = stats + summed(0)
+    rest_arrived(0)
+    table_sums = owned(0)
     arrived(1)
     stats = stats + summed(1)
     stats = stats[:, 0:8] + stats[:, 8:16] + stats[:, 16:24]
@@ -271,8 +288,7 @@
             rad_ref[r, q] = jnp.where(mask, rad, 0.0)
 
     rest_arrived(1)
-    rest_arrived(0)
-    table_sums = owned(1) + owned(0)
+    table_sums = table_sums + owned(1)
     own = table_sums[0:16] + table_sums[16:32] + table_sums[32:48]
     heavy = jnp.maximum(own[0:1], 1.0)
     c = [own[1 + i : 2 + i] / heavy for i in range(3)]
@@ -284,10 +300,6 @@
         own[11:12] / heavy - (c[0] * d[1] - c[1] * d[0]),
     ]
 
-    def served(r):
-        share = min(2, roots)
-        return [p for p in range(roots, depth) if roots - 1 - (p - roots) * share // (depth - roots) == r]
-
     def tell(there, a, k):
         return pltpu.make_async_remote_copy(
             line, line, send_sem.at[2], recv_sem.at[4],
@@ -300,17 +312,13 @@
         pltpu.make_async_copy(others, others, recv_sem.at[3]).wait()
         rows = masses[...].reshape(everyone // 8, 8, blocks)
         line[...] = jnp.sum(jnp.sum(rows, axis=0), axis=0, keepdims=True)
-        for a in range(planes_groups):
-            for k in range(domains):
-                if (a, k) != (0, ROOT):
-                    tell(z, a, k).start()
-        for r in range(roots):
-            @pl.when(z == r)
+
+    for mine, (_, clients) in zip(i_am, tree):
+        if clients:
+            @pl.when(mine)
             def _():
-                for there in served(r):
-                    for a in range(planes_groups):
-                        for k in range(domains):
-                            tell(there, a, k).start()
+                for client in clients:
+                    tell(*client).start()
 
     @pl.when(jnp.logical_not(is_root))
     def _():
@@ -322,18 +330,19 @@
 
     @pl.when(is_root)
     def _():
-        for r in range(roots):
-            @pl.when(z == r)
+        sent = masses.at[pl.ds(0, n_roots - 1)]
+        pltpu.make_async_copy(sent, sent, send_sem.at[0]).wait()
+
+    for mine, (_, clients) in zip(i_am, tree):
+        if clients:
+            @pl.when(mine)
             def _():
-                told = masses.at[pl.ds(0, (1 + len(served(r))) * planes_groups * domains - 1)]
+                told = masses.at[pl.ds(0, len(clients))]
                 pltpu.make_async_copy(told, told, send_sem.at[2]).wait()
-
-        sent = masses.at[pl.ds(0, roots - 1)]
-        pltpu.make_async_copy(sent, sent, send_sem.at[0]).wait()
 
     @pl.when(jnp.logical_not(is_root))
     def _():
-        sent = masses.at[pl.ds(0, roots)]
+        sent = masses.at[pl.ds(0, n_roots)]
         pltpu.make_async_copy(sent, sent, send_sem.at[0]).wait()
 
     n_near = len(near)

time: 20.3 us -> 19.7 us (0.970)
  Pallas kernels: 18.9 us -> 18.2 us
    pallas_call x1, Pallas kernels: 18.1 us -> 17.4 us  [local(): pl.pallas_call(functools.partial(kernel, (groups, domains, plane_groups))...]
where the time goes in v4:
time: 19.7 us; the launch traced here: 19.5 us
  Pallas kernels  18.2 us (92%)
  between operations  1.29 us (7%)
    pallas_call x1, Pallas kernels, local(): pl.pallas_call(functools.partial(kernel, (groups, domains, plane_groups))...  17.4 us
    pallas_call x1, Pallas kernels, local(): pl.pallas_call(flush, out_shape=tuple((jax.ShapeDtypeStruct(r.shape, F32)...  0.82 us

profile of v4, /device:TPU:1, one launch (start us, length us, event | category | flops | bytes accessed | tf_op | source)
XLA Modules:
  0.0 19.5 jit_solution(16616665702311687327)
XLA Ops:
  1.3 17.4 %shard_map.103 = (f32[11,128]{1,0:T(8,128)S(1)}, f32[128,512]{1,0:T(8,128)S(1)}, f32[128,512]{1,0:T(8,128)S(1)}) custom-call(f32[3,128,512]{2,1,0:T(8,128)} %pos_hbm.1, f32[3,128,512]{2,1,0:T(8,128)} %vel_hbm.1, f32[128,512]{1,0:T(8,128)} %mass_hbm.1, s32[1,128]{1,0:T(1,128)} %bitcast.6, s32[3,128]{1,0:T(4,128)} %shift_hbm.1, s32[1,128]{1,0:T(1,128)} %bitcast.7, ...), custom_call_target="tpu_custom_call" | custom-call | tf_op jit(solution)/shard_map/pallas_call | solution.py:373
  18.7 0.8 %shard_map.104 = (f32[11,128]{1,0:T(8,128)}, f32[128,512]{1,0:T(8,128)}, f32[128,512]{1,0:T(8,128)}) custom-call(f32[11,128]{1,0:T(8,128)S(1)} %get-tuple-element.6.table_ref, f32[128,512]{1,0:T(8,128)S(1)} %get-tuple-element.7.kin_ref, f32[128,512]{1,0:T(8,128)S(1)} %get-tuple-element.8.rad_ref), custom_call_target="tpu_custom_call" | custom-call | tf_op jit(solution)/shard_map/pallas_call | solution.py:412

commit v5 on v4

--- a/solution.py
+++ b/solution.py
@@ -32,10 +32,12 @@
 
 
 def roots_of(depth, planes_groups, domains):
-    half = depth // 2
-    second = (ROOT + 2) % domains if domains > 2 else 0
+    half = max(2, depth * 3 // 8)
     plane = [(a, k) for a in range(planes_groups) for k in range(domains)]
-    tree = [((0, 0, ROOT), []), ((0, 0, second), [(0, 0, k) for k in range(domains) if k not in (ROOT, second)])]
+    tree = [((0, 0, 0), []), ((0, 0, ROOT), [])]
+    if domains > 2:
+        tree.append(((0, 0, 3), [(0, 0, k) for k in range(2, domains - 2) if k != 3]))
+        tree.append(((0, 0, domains - 1), [(0, 0, domains - 2)]))
     tree += [((0, a, ROOT), [(0, a, k) for k in range(domains) if k != ROOT]) for a in range(1, planes_groups)]
     share = max(1, min(2, half - 1))
     for r in range(1, half):
@@ -49,7 +51,7 @@
     pos_hbm, vel_hbm, mass_hbm, halo_hbm, shift_hbm, live_hbm, count_hbm, slot_hbm,
     table_ref, kin_ref, rad_ref,
     pos, vel, mass, halo, shift, live, count, slots,
-    live_bc, halo_bc, shift_bc, moments, rest, gather, gather_rest, masses, line,
+    live_bc, halo_bc, shift_bc, moments, rest, gather, gather_rest, mine_all, masses, line,
     in_sem, small_sem, count_sem, send_sem, recv_sem,
 ):
     groups, domains, planes_groups = sizes
@@ -173,7 +175,9 @@
 
     moments[0:9, :] = jnp.concatenate([m[0], *place, *mom_v, m[7], halo_row], axis=0)
     gather[domains + j, 0:9, :] = moments[0:9, :]
-    masses[pl.ds(me, 1), :] = m[0]
+    whole = jnp.broadcast_to(jnp.sum(m[0], axis=1, keepdims=True), (1, blocks))
+    mine_all[...] = whole
+    masses[pl.ds(me, 1), :] = whole
 
     pl.semaphore_wait(barrier, jnp.where(is_root, len(near) + n_roots - 1, len(near) + n_roots))
 
@@ -181,7 +185,7 @@
         @pl.when(jnp.logical_not(mine))
         def _():
             pltpu.make_async_remote_copy(
-                moments.at[pl.ds(0, 1)], masses.at[pl.ds(me, 1)], send_sem.at[0], recv_sem.at[3],
+                mine_all, masses.at[pl.ds(me, 1)], send_sem.at[0], recv_sem.at[3],
                 device_id=(there * planes_groups + a, k), device_id_type=MESH,
             ).start()
 
@@ -265,7 +269,9 @@
     rest_arrived(0)
     table_sums = owned(0)
     arrived(1)
+    rest_arrived(1)
     stats = stats + summed(1)
+    table_sums = table_sums + owned(1)
     stats = stats[:, 0:8] + stats[:, 8:16] + stats[:, 16:24]
     wide = [jnp.broadcast_to(stats[:, k : k + 1], (blocks, 128)) for k in range(8)]
     heavy = 1.0 / jnp.maximum(wide[0], 1.0)
@@ -287,8 +293,6 @@
             kin_ref[r, q] = jnp.where(mask, kin, 0.0)
             rad_ref[r, q] = jnp.where(mask, rad, 0.0)
 
-    rest_arrived(1)
-    table_sums = table_sums + owned(1)
     own = table_sums[0:16] + table_sums[16:32] + table_sums[32:48]
     heavy = jnp.maximum(own[0:1], 1.0)
     c = [own[1 + i : 2 + i] / heavy for i in range(3)]
@@ -300,6 +304,24 @@
         own[11:12] / heavy - (c[0] * d[1] - c[1] * d[0]),
     ]
 
+    table_ref[1:11, :] = jnp.concatenate([*c, *d, spread, *spin], axis=0)
+
+    @pl.when(is_root)
+    def _():
+        sent = masses.at[pl.ds(0, n_roots - 1)]
+        pltpu.make_async_copy(sent, sent, send_sem.at[0]).wait()
+
+    @pl.when(jnp.logical_not(is_root))
+    def _():
+        sent = masses.at[pl.ds(0, n_roots)]
+        pltpu.make_async_copy(sent, sent, send_sem.at[0]).wait()
+
+    n_near = len(near)
+    sent = gather.at[pl.ds(0, n_near), pl.ds(0, 9)]
+    pltpu.make_async_copy(sent, sent, send_sem.at[1]).wait()
+    sent = gather_rest.at[pl.ds(0, 2 * domains - 1), pl.ds(0, 4)]
+    pltpu.make_async_copy(sent, sent, send_sem.at[3]).wait()
+
     def tell(there, a, k):
         return pltpu.make_async_remote_copy(
             line, line, send_sem.at[2], recv_sem.at[4],
@@ -324,14 +346,7 @@
     def _():
         pltpu.make_async_copy(line, line, recv_sem.at[4]).wait()
 
-    total = jnp.sum(line[...], axis=1, keepdims=True)
-    share = own[0:1] * float(groups * domains * blocks) / total
-    table_ref[...] = jnp.concatenate([share, *c, *d, spread, *spin], axis=0)
-
-    @pl.when(is_root)
-    def _():
-        sent = masses.at[pl.ds(0, n_roots - 1)]
-        pltpu.make_async_copy(sent, sent, send_sem.at[0]).wait()
+    table_ref[0:1, :] = own[0:1] * float(groups * domains * blocks) / line[...]
 
     for mine, (_, clients) in zip(i_am, tree):
         if clients:
@@ -339,17 +354,6 @@
             def _():
                 told = masses.at[pl.ds(0, len(clients))]
                 pltpu.make_async_copy(told, told, send_sem.at[2]).wait()
-
-    @pl.when(jnp.logical_not(is_root))
-    def _():
-        sent = masses.at[pl.ds(0, n_roots)]
-        pltpu.make_async_copy(sent, sent, send_sem.at[0]).wait()
-
-    n_near = len(near)
-    sent = gather.at[pl.ds(0, n_near), pl.ds(0, 9)]
-    pltpu.make_async_copy(sent, sent, send_sem.at[1]).wait()
-    sent = gather_rest.at[pl.ds(0, 2 * domains - 1), pl.ds(0, 4)]
-    pltpu.make_async_copy(sent, sent, send_sem.at[3]).wait()
 
 
 def flush(table_ref, kin_ref, rad_ref, table_hbm, kin_hbm, rad_hbm, sem):
@@ -395,6 +399,7 @@
                 pltpu.VMEM((8, blocks), F32),
                 pltpu.VMEM((3 * domains, 16, blocks), F32),
                 pltpu.VMEM((2 * domains, 8, blocks), F32),
+                pltpu.VMEM((1, blocks), F32),
                 pltpu.VMEM((groups * domains, blocks), F32),
                 pltpu.VMEM((1, blocks), F32),
                 pltpu.SemaphoreType.DMA((3 * CHUNKS,)),

time: 19.7 us -> 19.5 us (0.990)
  no operation moved by 1% of the time
where the time goes in v5:
time: 19.5 us; the launch traced here: 19.4 us
  Pallas kernels  18.1 us (93%)
  between operations  1.29 us (7%)
    pallas_call x1, Pallas kernels, local(): pl.pallas_call(functools.partial(kernel, (groups, domains, plane_groups))...  17.2 us
    pallas_call x1, Pallas kernels, local(): pl.pallas_call(flush, out_shape=tuple((jax.ShapeDtypeStruct(r.shape, F32)...  0.82 us

profile of v5, /device:TPU:1, one launch (start us, length us, event | category | flops | bytes accessed | tf_op | source)
XLA Modules:
  0.0 19.4 jit_solution(7593288634118849105)
XLA Ops:
  1.3 17.2 %shard_map.103 = (f32[11,128]{1,0:T(8,128)S(1)}, f32[128,512]{1,0:T(8,128)S(1)}, f32[128,512]{1,0:T(8,128)S(1)}) custom-call(f32[3,128,512]{2,1,0:T(8,128)} %pos_hbm.1, f32[3,128,512]{2,1,0:T(8,128)} %vel_hbm.1, f32[128,512]{1,0:T(8,128)} %mass_hbm.1, s32[1,128]{1,0:T(1,128)} %bitcast.6, s32[3,128]{1,0:T(4,128)} %shift_hbm.1, s32[1,128]{1,0:T(1,128)} %bitcast.7, ...), custom_call_target="tpu_custom_call" | custom-call | tf_op jit(solution)/shard_map/pallas_call | solution.py:377
  18.5 0.8 %shard_map.104 = (f32[11,128]{1,0:T(8,128)}, f32[128,512]{1,0:T(8,128)}, f32[128,512]{1,0:T(8,128)}) custom-call(f32[11,128]{1,0:T(8,128)S(1)} %get-tuple-element.6.table_ref, f32[128,512]{1,0:T(8,128)S(1)} %get-tuple-element.7.kin_ref, f32[128,512]{1,0:T(8,128)S(1)} %get-tuple-element.8.rad_ref), custom_call_target="tpu_custom_call" | custom-call | tf_op jit(solution)/shard_map/pallas_call | solution.py:417

commit v6 on v5

--- a/solution.py
+++ b/solution.py
@@ -103,8 +103,22 @@
     for copy in small[2:]:
         copy.start()
     barrier = pltpu.get_barrier_semaphore()
-    for grp, k, _ in near:
-        greet(grp, domain(k))
+    first, last = g == 0, x == planes_groups - 1
+
+    @pl.when(x == 0)
+    def _():
+        for k in order:
+            greet(prv, domain(k))
+
+    @pl.when(jnp.logical_not(last) | (g != groups - 1))
+    def _():
+        for k in order:
+            greet(nxt, domain(k))
+
+    for k in order:
+        if k:
+            greet(g, domain(k))
+
 
     @pl.when(is_root)
     def _():
@@ -179,7 +193,8 @@
     mine_all[...] = whole
     masses[pl.ds(me, 1), :] = whole
 
-    pl.semaphore_wait(barrier, jnp.where(is_root, len(near) + n_roots - 1, len(near) + n_roots))
+    heard = jnp.where(first, 0, domains) + jnp.where(last, domains, 0) + jnp.where(is_root, n_roots - 1, n_roots)
+    pl.semaphore_wait(barrier, domains - 1 + heard)
 
     for mine, ((there, a, k), _) in zip(i_am, tree):
         @pl.when(jnp.logical_not(mine))
@@ -189,11 +204,32 @@
                 device_id=(there * planes_groups + a, k), device_id_type=MESH,
             ).start()
 
-    for grp, k, d in near:
-        pltpu.make_async_remote_copy(
-            moments.at[pl.ds(0, 9)], gather.at[d * domains + j, pl.ds(0, 9)], send_sem.at[1], recv_sem.at[d],
-            device_id=(grp, domain(k)), device_id_type=MESH,
-        ).start()
+    def send(d):
+        for grp, k, kind in near:
+            if kind == d:
+                pltpu.make_async_remote_copy(
+                    moments.at[pl.ds(0, 9)], gather.at[d * domains + j, pl.ds(0, 9)], send_sem.at[1], recv_sem.at[d],
+                    device_id=(grp, domain(k)), device_id_type=MESH,
+                ).start()
+
+    def send_rest(d):
+        for grp, k, kind in near:
+            if kind == d:
+                pltpu.make_async_remote_copy(
+                    rest.at[pl.ds(0, 4)], gather_rest.at[d * domains + j, pl.ds(0, 4)], send_sem.at[3], recv_sem.at[5 + d],
+                    device_id=(grp, domain(k)), device_id_type=MESH,
+                ).start()
+
+    @pl.when(last)
+    def _():
+        send(0)
+
+    @pl.when(jnp.logical_not(first))
+    def _():
+        send(2)
+
+    send(1)
+
     halo_int = halo[...]
     high_bits = halo_int // 128
     low_bits = halo_int - high_bits * 128
@@ -214,12 +250,13 @@
 
     rest[0:4, :] = jnp.concatenate([slot_row, *ang], axis=0)
     gather_rest[domains + j, 0:4, :] = rest[0:4, :]
-    for grp, k, d in near:
-        if d < 2:
-            pltpu.make_async_remote_copy(
-                rest.at[pl.ds(0, 4)], gather_rest.at[d * domains + j, pl.ds(0, 4)], send_sem.at[3], recv_sem.at[5 + d],
-                device_id=(grp, domain(k)), device_id_type=MESH,
-            ).start()
+
+    @pl.when(last)
+    def _():
+        send_rest(0)
+
+    send_rest(1)
+
     halo_bc[...] = jnp.broadcast_to(halo_row, (blocks, blocks)).T
     for c in range(3):
         shift_bc[c] = jnp.broadcast_to(s[c], (blocks, blocks)).T
@@ -263,15 +300,24 @@
         )
 
     arrived(2)
+
+    @pl.when(jnp.logical_not(last))
+    def _():
+        send(0)
+        send_rest(0)
+
     stats = summed(2)
-    arrived(0)
-    stats = stats + summed(0)
-    rest_arrived(0)
-    table_sums = owned(0)
     arrived(1)
     rest_arrived(1)
     stats = stats + summed(1)
-    table_sums = table_sums + owned(1)
+    table_sums = owned(1)
+    arrived(0)
+
+    @pl.when(first)
+    def _():
+        send(2)
+
+    stats = stats + summed(0)
     stats = stats[:, 0:8] + stats[:, 8:16] + stats[:, 16:24]
     wide = [jnp.broadcast_to(stats[:, k : k + 1], (blocks, 128)) for k in range(8)]
     heavy = 1.0 / jnp.maximum(wide[0], 1.0)
@@ -293,6 +339,8 @@
             kin_ref[r, q] = jnp.where(mask, kin, 0.0)
             rad_ref[r, q] = jnp.where(mask, rad, 0.0)
 
+    rest_arrived(0)
+    table_sums = table_sums + owned(0)
     own = table_sums[0:16] + table_sums[16:32] + table_sums[32:48]
     heavy = jnp.maximum(own[0:1], 1.0)
     c = [own[1 + i : 2 + i] / heavy for i in range(3)]

time: 19.5 us -> 19.2 us (0.985)
  Pallas kernels: 18.1 us -> 17.8 us
    pallas_call x1, Pallas kernels: 17.2 us -> 17 us  [local(): pl.pallas_call(functools.partial(kernel, (groups, domains, plane_groups))...]
where the time goes in v6:
time: 19.2 us; the launch traced here: 19.1 us
  Pallas kernels  17.8 us (93%)
  between operations  1.29 us (7%)
    pallas_call x1, Pallas kernels, local(): pl.pallas_call(functools.partial(kernel, (groups, domains, plane_groups))...  17 us
    pallas_call x1, Pallas kernels, local(): pl.pallas_call(flush, out_shape=tuple((jax.ShapeDtypeStruct(r.shape, F32)...  0.82 us

profile of v6, /device:TPU:1, one launch (start us, length us, event | category | flops | bytes accessed | tf_op | source)
XLA Modules:
  0.0 19.1 jit_solution(4081766471950358658)
XLA Ops:
  1.3 17.0 %shard_map.103 = (f32[11,128]{1,0:T(8,128)S(1)}, f32[128,512]{1,0:T(8,128)S(1)}, f32[128,512]{1,0:T(8,128)S(1)}) custom-call(f32[3,128,512]{2,1,0:T(8,128)} %pos_hbm.1, f32[3,128,512]{2,1,0:T(8,128)} %vel_hbm.1, f32[128,512]{1,0:T(8,128)} %mass_hbm.1, s32[1,128]{1,0:T(1,128)} %bitcast.6, s32[3,128]{1,0:T(4,128)} %shift_hbm.1, s32[1,128]{1,0:T(1,128)} %bitcast.7, ...), custom_call_target="tpu_custom_call" | custom-call | tf_op jit(solution)/shard_map/pallas_call | solution.py:425
  18.3 0.8 %shard_map.104 = (f32[11,128]{1,0:T(8,128)}, f32[128,512]{1,0:T(8,128)}, f32[128,512]{1,0:T(8,128)}) custom-call(f32[11,128]{1,0:T(8,128)S(1)} %get-tuple-element.6.table_ref, f32[128,512]{1,0:T(8,128)S(1)} %get-tuple-element.7.kin_ref, f32[128,512]{1,0:T(8,128)S(1)} %get-tuple-element.8.rad_ref), custom_call_target="tpu_custom_call" | custom-call | tf_op jit(solution)/shard_map/pallas_call | solution.py:465

commit v7 on v6

--- a/solution.py
+++ b/solution.py
@@ -105,19 +105,19 @@
     barrier = pltpu.get_barrier_semaphore()
     first, last = g == 0, x == planes_groups - 1
 
-    @pl.when(x == 0)
-    def _():
-        for k in order:
-            greet(prv, domain(k))
-
-    @pl.when(jnp.logical_not(last) | (g != groups - 1))
-    def _():
-        for k in order:
-            greet(nxt, domain(k))
-
     for k in order:
         if k:
             greet(g, domain(k))
+
+    @pl.when(x == 0)
+    def _():
+        for k in order:
+            greet(prv, domain(k))
+
+    @pl.when(jnp.logical_not(last) | (g != groups - 1))
+    def _():
+        for k in order:
+            greet(nxt, domain(k))
 
 
     @pl.when(is_root)

time: 19.2 us -> 19.2 us (level)
  no operation moved by 1% of the time
where the time goes in v7:
time: 19.2 us; the launch traced here: 19.1 us
  Pallas kernels  17.8 us (93%)
  between operations  1.29 us (7%)
    pallas_call x1, Pallas kernels, local(): pl.pallas_call(functools.partial(kernel, (groups, domains, plane_groups))...  17 us
    pallas_call x1, Pallas kernels, local(): pl.pallas_call(flush, out_shape=tuple((jax.ShapeDtypeStruct(r.shape, F32)...  0.82 us

profile of v7, /device:TPU:1, one launch (start us, length us, event | category | flops | bytes accessed | tf_op | source)
XLA Modules:
  0.0 19.1 jit_solution(7439897908215140617)
XLA Ops:
  1.3 17.0 %shard_map.103 = (f32[11,128]{1,0:T(8,128)S(1)}, f32[128,512]{1,0:T(8,128)S(1)}, f32[128,512]{1,0:T(8,128)S(1)}) custom-call(f32[3,128,512]{2,1,0:T(8,128)} %pos_hbm.1, f32[3,128,512]{2,1,0:T(8,128)} %vel_hbm.1, f32[128,512]{1,0:T(8,128)} %mass_hbm.1, s32[1,128]{1,0:T(1,128)} %bitcast.6, s32[3,128]{1,0:T(4,128)} %shift_hbm.1, s32[1,128]{1,0:T(1,128)} %bitcast.7, ...), custom_call_target="tpu_custom_call" | custom-call | tf_op jit(solution)/shard_map/pallas_call | solution.py:425
  18.3 0.8 %shard_map.104 = (f32[11,128]{1,0:T(8,128)}, f32[128,512]{1,0:T(8,128)}, f32[128,512]{1,0:T(8,128)}) custom-call(f32[11,128]{1,0:T(8,128)S(1)} %get-tuple-element.6.table_ref, f32[128,512]{1,0:T(8,128)S(1)} %get-tuple-element.7.kin_ref, f32[128,512]{1,0:T(8,128)S(1)} %get-tuple-element.8.rad_ref), custom_call_target="tpu_custom_call" | custom-call | tf_op jit(solution)/shard_map/pallas_call | solution.py:465
